TPU v7x, 32 devices: a whole 2x2x4 slice. The times are simulated.
32 devices in a mesh: dp: 4 (over y, x), expert: 8 (over z, core).
Axes of the slice: x: 2, y: 2, z: 4, core: 2. Of those that a mesh axis runs over, the one named last changes fastest.
Arguments:
- inputs: bfloat16 [16384, 768], P(('dp', 'expert')), may hold values from -6 to 6
- cotangent: bfloat16 [16384, 768], P(('dp', 'expert')), may hold values from -6 to 6
- lengths: int32 [32], P(('dp', 'expert')), may hold values from 384 to 512, as said below
- routes: int32 [16384, 2], P(('dp', 'expert')), may hold values from 0 to 7, all different within a row; in each aligned block of 512 rows (0 to 511, 512 to 1023, ...) at most 192 rows name the same one
- w_qkv: bfloat16 [768, 2304], P('dp'), may hold values from -0.21875 to 0.21875
- w_attn_out: bfloat16 [768, 768], P('dp'), may hold values from -1.25 to 1.25
- w_router: bfloat16 [768, 8], P('dp'), may hold values from -0.4375 to 0.4375
- gain_attn: bfloat16 [768], P('dp'), may hold values from 0.5 to 1.5
- gain_moe: bfloat16 [768], P('dp'), may hold values from 0.5 to 1.5
- rel_bias: bfloat16 [12, 32], P('dp'), may hold values from -4 to 4
- w_in: bfloat16 [8, 768, 3072], P('expert'), may hold values from -0.21875 to 0.21875
- w_out: bfloat16 [8, 768, 3072], P('expert'), may hold values from -0.109375 to 0.109375
Outputs:
- outputs: bfloat16 [16384, 768], P(('dp', 'expert'))
- d_inputs: bfloat16 [16384, 768], P(('dp', 'expert'))
- grad_qkv: float32 [768, 2304], P('dp')
- grad_attn_out: float32 [768, 768], P('dp')
- grad_router: float32 [768, 8], P('dp')
- grad_gain_attn: float32 [768], P('dp')
- grad_gain_moe: float32 [768], P('dp')
- grad_rel_bias: float32 [12, 32], P('dp')
- grad_w_in: float32 [8, 768, 3072], P('expert', None, 'dp')
- grad_w_out: float32 [8, 768, 3072], P('expert', None, 'dp')
Inputs may be any that keep to these rules, and one draw needn't show every extreme that they name: `lengths`: slots of a sequence at or past its length are padding; some sequence is full and some has the fewest valid tokens. `routes`: a token names two different experts; in the rows of one device no expert is named more than 192 times, a bound that some block reaches.
All inputs are finite; a program needn't handle non-finite values.
Results may differ from a plain program's by a relative error of at most 0.018.
Values may be sent and summed in bfloat16 or wider, within the bound.
A program may use at most 256 MiB of HBM per device.

v0:
```python
import jax
import jax.numpy as jnp
from jax import lax
from jax.sharding import PartitionSpec as P

norm_eps = 1e-06
rel_edges = (19, 21, 24, 27, 31, 35, 40, 46, 52, 59, 67, 77, 87, 99, 113)


def rms_apply(vector, gain_vec):
    return (
        vector * lax.rsqrt(jnp.mean(vector * vector, axis=-1, keepdims=True) + norm_eps) * gain_vec
    )


def bucket_of(distance):
    far_bucket = jnp.full(distance.shape, 16, jnp.int32)
    for edge_value in rel_edges:
        far_bucket = far_bucket + (distance >= edge_value).astype(jnp.int32)
    return jnp.where(distance < 16, distance, far_bucket)


def on_device(
    inputs,
    cotangent,
    lengths,
    routes,
    w_qkv,
    w_attn_out,
    w_router,
    gain_attn,
    gain_moe,
    rel_bias,
    w_in,
    w_out,
):
    w_proj, w_mix, w_gate, gain_one, gain_two, bias_table = (
        lax.all_gather(w_qkv, "dp", axis=0, tiled=True),
        lax.all_gather(w_attn_out, "dp", axis=0, tiled=True),
        lax.all_gather(w_router, "dp", axis=0, tiled=True),
        lax.all_gather(gain_attn, "dp", axis=0, tiled=True),
        lax.all_gather(gain_moe, "dp", axis=0, tiled=True),
        lax.all_gather(rel_bias, "dp", axis=0, tiled=True),
    )
    tok_count, model_width = inputs.shape
    head_count, bucket_count = bias_table.shape
    head_size = model_width // head_count
    top_count = routes.shape[1]
    expert_count = w_gate.shape[1]
    local_count = w_in.shape[0]
    group_count = expert_count // local_count
    capacity = 3 * tok_count * top_count // (2 * expert_count)
    block_rows = min(512, tok_count)
    block_count = tok_count // block_rows
    score_scale = head_size ** (-0.5)
    positions = jnp.arange(tok_count, dtype=jnp.int32)
    valid_mask = (positions < lengths[0]).astype(jnp.float32)
    inputs_wide = inputs.astype(jnp.float32)
    gain_first = gain_one.astype(jnp.float32)
    gain_second = gain_two.astype(jnp.float32)
    normed_attn = rms_apply(inputs_wide, gain_first).astype(jnp.bfloat16)
    proj_qkv = jnp.dot(normed_attn, w_proj, preferred_element_type=jnp.float32).astype(jnp.bfloat16)
    query_heads = proj_qkv[:, :model_width].reshape(tok_count, head_count, head_size)
    key_heads = proj_qkv[:, model_width : 2 * model_width].reshape(tok_count, head_count, head_size)
    value_heads = proj_qkv[:, 2 * model_width :].reshape(tok_count, head_count, head_size)
    bucket_ids = jnp.arange(bucket_count, dtype=jnp.int32)

    def scores_of(row_start):
        distance = (row_start + jnp.arange(block_rows, dtype=jnp.int32))[:, None] - positions[
            None, :
        ]
        allowed = (distance >= 0) & (positions[None, :] < lengths[0])
        one_hot = (bucket_of(jnp.maximum(distance, 0))[:, :, None] == bucket_ids).astype(
            jnp.bfloat16
        )
        bias_term = jnp.einsum(
            "hb,qkb->hqk", bias_table, one_hot, preferred_element_type=jnp.float32
        )
        raw_scores = (
            jnp.einsum("qhd,khd->hqk", query_heads, key_heads, preferred_element_type=jnp.float32)
            * score_scale
            + bias_term
        )
        return (query_heads, one_hot, jnp.where(allowed[None], raw_scores, -1e30))

    def forward_block(block_index):
        row_start = block_index * block_rows
        query_block, one_hot, raw_scores = scores_of(row_start)
        top_score = jnp.max(raw_scores, axis=-1, keepdims=True)
        exp_terms = jnp.exp(raw_scores - top_score)
        row_total = jnp.sum(exp_terms, axis=-1, keepdims=True)
        attn_prob = (exp_terms / row_total).astype(jnp.bfloat16)
        head_out = jnp.einsum(
            "hqk,khd->qhd", attn_prob, value_heads, preferred_element_type=jnp.float32
        )
        return (
            head_out.reshape(block_rows, model_width).astype(jnp.bfloat16),
            top_score[..., 0] + jnp.log(row_total[..., 0]),
        )

    attn_heads, log_totals = lax.map(forward_block, jnp.arange(block_count, dtype=jnp.int32))
    attn_heads = attn_heads.reshape(tok_count, model_width)
    attn_proj = jnp.dot(attn_heads, w_mix, preferred_element_type=jnp.float32)
    hidden = inputs_wide + valid_mask[:, None] * attn_proj
    normed_moe = rms_apply(hidden, gain_second).astype(jnp.bfloat16)
    logits = jnp.dot(normed_moe, w_gate, preferred_element_type=jnp.float32)
    expert_ids = jnp.arange(expert_count, dtype=jnp.int32)
    chosen_mask = (routes[:, :, None] == expert_ids).astype(jnp.float32)
    chosen = jnp.sum(logits[:, None, :] * chosen_mask, axis=-1)
    gate_pair = jax.nn.softmax(chosen, axis=-1)
    gate_used = gate_pair * valid_mask[:, None]
    flat_routes = routes.reshape(-1)
    flat_valid = jnp.broadcast_to(valid_mask[:, None], routes.shape).reshape(-1) > 0
    route_hot = ((flat_routes[:, None] == expert_ids) & flat_valid[:, None]).astype(jnp.int32)
    rank_in = jnp.sum((jnp.cumsum(route_hot, axis=0) - route_hot) * route_hot, axis=1)
    slot_index = jnp.where(flat_valid, flat_routes * capacity + rank_in, expert_count * capacity)
    route_ids = jnp.arange(tok_count * top_count, dtype=jnp.int32)
    source = jnp.zeros((expert_count * capacity + 1,), jnp.int32).at[slot_index].set(route_ids)[:-1]
    filled = jnp.zeros((expert_count * capacity + 1,), jnp.bfloat16).at[slot_index].set(1)[:-1]
    send_rows = (normed_moe[source // top_count] * filled[:, None]).reshape(
        group_count, local_count, capacity, model_width
    )
    recv_rows = lax.all_to_all(send_rows, "expert", split_axis=0, concat_axis=0, tiled=True)
    pre_act = jnp.einsum("nekd,edf->nekf", recv_rows, w_in, preferred_element_type=jnp.float32)
    activation = jax.nn.gelu(pre_act).astype(jnp.bfloat16)
    expert_out = jnp.einsum(
        "nekf,edf->nekd", activation, w_out, preferred_element_type=jnp.float32
    ).astype(jnp.bfloat16)
    returned = lax.all_to_all(expert_out, "expert", split_axis=0, concat_axis=0, tiled=True)
    results = (returned, recv_rows, pre_act)
    returned = results[0]
    kept_rows = results[1]
    out_table = jnp.concatenate(
        [
            returned.reshape(expert_count * capacity, model_width),
            jnp.zeros((1, model_width), jnp.bfloat16),
        ],
        axis=0,
    )
    picked = out_table[slot_index].reshape(tok_count, top_count, model_width).astype(jnp.float32)
    moe_out = jnp.sum(gate_used[:, :, None] * picked, axis=1)
    outputs = (valid_mask[:, None] * (hidden + moe_out)).astype(jnp.bfloat16)
    grad_out = cotangent.astype(jnp.float32) * valid_mask[:, None]
    d_gate = jnp.sum(grad_out[:, None, :] * picked, axis=-1) * valid_mask[:, None]
    d_chosen = gate_pair * (d_gate - jnp.sum(gate_pair * d_gate, axis=-1, keepdims=True))
    d_logits = jnp.sum(d_chosen[:, :, None] * chosen_mask, axis=1).astype(jnp.bfloat16)
    grad_router = jnp.dot(normed_moe.T, d_logits, preferred_element_type=jnp.float32)
    d_normed = jnp.dot(d_logits, w_gate.T, preferred_element_type=jnp.float32)
    route_weight = gate_used.reshape(-1)
    d_send = (
        grad_out[source // top_count] * (route_weight[source] * filled.astype(jnp.float32))[:, None]
    ).astype(jnp.bfloat16)
    d_send = d_send.reshape(group_count, local_count, capacity, model_width)
    d_recv = lax.all_to_all(d_send, "expert", split_axis=0, concat_axis=0, tiled=True)
    pre_act = results[2]
    act_full, gelu_back = jax.vjp(jax.nn.gelu, pre_act)
    activation = act_full.astype(jnp.bfloat16)
    d_act = jnp.einsum("nekd,edf->nekf", d_recv, w_out, preferred_element_type=jnp.float32)
    d_pre = gelu_back(d_act)[0].astype(jnp.bfloat16)
    full_w_out = jnp.einsum(
        "nekd,nekf->edf", d_recv, activation, preferred_element_type=jnp.float32
    )
    full_w_in = jnp.einsum("nekd,nekf->edf", kept_rows, d_pre, preferred_element_type=jnp.float32)
    d_rows = jnp.einsum("nekf,edf->nekd", d_pre, w_in, preferred_element_type=jnp.float32).astype(
        jnp.bfloat16
    )
    d_returned = lax.all_to_all(d_rows, "expert", split_axis=0, concat_axis=0, tiled=True)
    grad_w_in, grad_w_out = (
        lax.psum_scatter(
            full_w_in.astype(jnp.bfloat16), "dp", scatter_dimension=2, tiled=True
        ).astype(jnp.float32),
        lax.psum_scatter(
            full_w_out.astype(jnp.bfloat16), "dp", scatter_dimension=2, tiled=True
        ).astype(jnp.float32),
    )
    d_table = jnp.concatenate(
        [
            d_returned.reshape(expert_count * capacity, model_width),
            jnp.zeros((1, model_width), jnp.bfloat16),
        ],
        axis=0,
    )
    d_normed = d_normed + jnp.sum(
        d_table[slot_index].reshape(tok_count, top_count, model_width).astype(jnp.float32), axis=1
    )
    second_val, second_back = jax.vjp(rms_apply, hidden, gain_second)
    d_hidden_norm, grad_gain_moe = second_back(d_normed)
    d_hidden = grad_out + d_hidden_norm
    d_attn_proj = (d_hidden * valid_mask[:, None]).astype(jnp.bfloat16)
    grad_attn_out = jnp.dot(attn_heads.T, d_attn_proj, preferred_element_type=jnp.float32)
    d_heads = (
        jnp.dot(d_attn_proj, w_mix.T, preferred_element_type=jnp.float32)
        .astype(jnp.bfloat16)
        .reshape(tok_count, head_count, head_size)
    )

    def backward_block(carry, block_index):
        d_keys, d_values, d_bias = carry
        row_start = block_index * block_rows
        query_block, one_hot, raw_scores = scores_of(row_start)
        attn_full = jnp.exp(raw_scores - log_totals[block_index][..., None])
        attn_prob = attn_full.astype(jnp.bfloat16)
        d_values = d_values + jnp.einsum(
            "hqk,qhd->khd", attn_prob, d_heads, preferred_element_type=jnp.float32
        )
        d_prob = jnp.einsum(
            "qhd,khd->hqk", d_heads, value_heads, preferred_element_type=jnp.float32
        )
        d_scores = (
            attn_full * (d_prob - jnp.sum(attn_full * d_prob, axis=-1, keepdims=True))
        ).astype(jnp.bfloat16)
        d_query = (
            jnp.einsum("hqk,khd->qhd", d_scores, key_heads, preferred_element_type=jnp.float32)
            * score_scale
        )
        d_keys = (
            d_keys
            + jnp.einsum("hqk,qhd->khd", d_scores, query_block, preferred_element_type=jnp.float32)
            * score_scale
        )
        d_bias = d_bias + jnp.einsum(
            "hqk,qkb->hb", d_scores, one_hot, preferred_element_type=jnp.float32
        )
        return ((d_keys, d_values, d_bias), d_query)

    start_carry = (
        jnp.zeros((tok_count, head_count, head_size), jnp.float32),
        jnp.zeros((tok_count, head_count, head_size), jnp.float32),
        jnp.zeros((head_count, bucket_count), jnp.float32),
    )
    final_carry, d_queries = lax.scan(
        backward_block, start_carry, jnp.arange(block_count, dtype=jnp.int32)
    )
    d_keys, d_values, grad_rel_bias = final_carry
    d_qkv = jnp.concatenate(
        [
            d_queries.reshape(tok_count, model_width),
            d_keys.reshape(tok_count, model_width),
            d_values.reshape(tok_count, model_width),
        ],
        axis=1,
    ).astype(jnp.bfloat16)
    grad_qkv = jnp.dot(normed_attn.T, d_qkv, preferred_element_type=jnp.float32)
    d_normed_attn = jnp.dot(d_qkv, w_proj.T, preferred_element_type=jnp.float32)
    first_val, first_back = jax.vjp(rms_apply, inputs_wide, gain_first)
    d_norm_in, grad_gain_attn = first_back(d_normed_attn)
    d_inputs = (d_hidden + d_norm_in).astype(jnp.bfloat16)
    summed = lax.psum(
        (grad_qkv, grad_attn_out, grad_router, grad_gain_attn, grad_gain_moe, grad_rel_bias),
        "expert",
    )
    shares = (
        lax.psum_scatter(
            summed[0].astype(jnp.bfloat16), "dp", scatter_dimension=0, tiled=True
        ).astype(jnp.float32),
        lax.psum_scatter(
            summed[1].astype(jnp.bfloat16), "dp", scatter_dimension=0, tiled=True
        ).astype(jnp.float32),
        lax.psum_scatter(
            summed[2].astype(jnp.bfloat16), "dp", scatter_dimension=0, tiled=True
        ).astype(jnp.float32),
        lax.psum_scatter(
            summed[3].astype(jnp.bfloat16), "dp", scatter_dimension=0, tiled=True
        ).astype(jnp.float32),
        lax.psum_scatter(
            summed[4].astype(jnp.bfloat16), "dp", scatter_dimension=0, tiled=True
        ).astype(jnp.float32),
        lax.psum_scatter(
            summed[5].astype(jnp.bfloat16), "dp", scatter_dimension=0, tiled=True
        ).astype(jnp.float32),
    )
    return (
        outputs,
        d_inputs,
        shares[0],
        shares[1],
        shares[2],
        shares[3],
        shares[4],
        shares[5],
        grad_w_in,
        grad_w_out,
    )


def solution(mesh):
    placed = (
        P(("dp", "expert"), None),
        P(("dp", "expert"), None),
        P(("dp", "expert")),
        P(("dp", "expert"), None),
        P("dp", None),
        P("dp", None),
        P("dp", None),
        P("dp"),
        P("dp"),
        P("dp", None),
        P("expert", None, None),
        P("expert", None, None),
    )
    return jax.shard_map(
        on_device,
        mesh=mesh,
        in_specs=placed,
        out_specs=(
            P(("dp", "expert"), None),
            P(("dp", "expert"), None),
            P("dp", None),
            P("dp", None),
            P("dp", None),
            P("dp"),
            P("dp"),
            P("dp", None),
            P("expert", None, "dp"),
            P("expert", None, "dp"),
        ),
        check_vma=False,
    )
```

profile of v0, /device:TPU:0, one launch (start us, length us, event | category | flops | bytes accessed | tf_op | source)
XLA Modules:
  0.0 836.9 jit_solution(11482958832264062407)
XLA Ops:
  14.5 11.6 %all-reduce.9 = (bf16[768]{0:T(1024)(128)(2,1)S(1)}, bf16[768]{0:T(1024)(128)(2,1)S(1)}) all-reduce(bf16[768]{0:T(1024)(128)(2,1)S(1)} %dynamic-update-slice, bf16[768]{0:T(1024)(128)(2,1)S(1)} %dynamic-update-slice.1), channel_id=1, replica_groups=mesh['dp'=4,'expert'=8] {'dp'}, use_global_device_ids=true, to_apply=%add.2 | all-reduce | flops 1536 | bytes 6144
  26.0 7.3 all-gather
  37.0 7.6 scatter_custom_fusion.1
  44.7 4.5 scatter_custom_fusion
  49.2 8.5 %fusion.1 = f32[512,512,12]{0,2,1:T(8,128)} fusion(bf16[12,32,1]{1,0,2:T(8,128)(2,1)S(1)} %reshape.597, s32[512,512]{0,1:T(8,128)S(1)} %compare_select_fusion), kind=kOutput, calls=%fused_computation.9 | convolution fusion | flops 209715200 | bytes 13632256 | tf_op jit(solution)/shard_map/while/body/eval_jaxpr/hb,qkb->hqk/dot_general | solution.py:76
  59.8 4.1 convolution_convert_fusion
  66.9 15.6 %fusion.132 = (f32[12,512]{1,0:T(8,128)S(1)}, f32[12,512,512]{1,2,0:T(8,128)S(1)}) fusion(f32[512,512,12]{0,2,1:T(8,128)} %fusion.1, bf16[512,12,64]{0,2,1:T(8,128)(2,1)S(1)} %bitcast.217, bf16[512,12,64]{0,2,1:T(8,128)(2,1)S(1)} %bitcast.212, pred[512,512]{0,1:T(8,128)(4,1)S(1)} %fusion.93), kind=kOutput, calls=%fused_computation.192 | convolution fusion | flops 415229952 | bytes 27025408 | tf_op jit(solution)/shard_map/while/body/eval_jaxpr/qhd,khd->hqk/dot_general | solution.py:80
  87.4 7.1 fusion.72
  98.5 5.0 gather_fusion
  105.1 4.8 all-to-all-start
  109.9 8.1 all-gather.1
  118.4 5.6 gather_fusion.2
  124.7 5.9 gather_fusion.3
  130.6 4.1 multiply_convert_fusion.1
  134.7 29.9 %all-to-all-done = bf16[8,1,192,768]{3,2,1,0:T(8,128)(2,1)} async-done(((bf16[8,1,192,768]{3,2,1,0:T(8,128)(2,1)}), bf16[8,1,192,768]{3,2,1,0:T(8,128)(2,1)}, u32[]{:S(2)}, u32[]{:S(2)}) %all-to-all-start) | async-done | bytes 2359328 | tf_op jit(solution)/shard_map/all_to_all | solution.py:123
  164.6 4.8 all-to-all-start.2
  169.4 13.7 %fusion.38 = f32[8,192,3072]{2,1,0:T(8,128)} fusion(bf16[1,768,3072]{2,1,0:T(8,128)(2,1)} %param.22, bf16[8,1,192,768]{3,2,1,0:T(8,128)(2,1)} %all-to-all-done), kind=kOutput, calls=%fused_computation.54 | convolution fusion | flops 7247757312 | bytes 25952256 | tf_op jit(solution)/shard_map/nekd,edf->nekf/dot_general | solution.py:124
  183.1 17.4 %convert_bitcast_fusion.1 = bf16[8,1,192,768]{3,2,1,0:T(8,128)(2,1)} fusion(bf16[1,768,3072]{2,1,0:T(8,128)(2,1)} %param.23, f32[8,192,3072]{2,1,0:T(8,128)} %fusion.38), kind=kOutput, calls=%fused_computation.76 | convolution fusion | flops 7291404288 | bytes 25952256 | tf_op jit(solution)/shard_map/nekf,edf->nekd/dot_general | solution.py:126
  200.5 23.6 %all-to-all-done.2 = bf16[8,1,192,768]{3,2,1,0:T(8,128)(2,1)} async-done(((bf16[8,1,192,768]{3,2,1,0:T(8,128)(2,1)}), bf16[8,1,192,768]{3,2,1,0:T(8,128)(2,1)}, u32[]{:S(2)}, u32[]{:S(2)}) %all-to-all-start.2) | async-done | bytes 2359328 | tf_op jit(solution)/shard_map/all_to_all | solution.py:154
  224.1 4.5 all-to-all-start.1
  228.6 22.0 %fusion.8 = bf16[8,1,192,3072]{3,2,0,1:T(8,128)(2,1)S(1)} fusion(f32[8,192,3072]{2,1,0:T(8,128)} %fusion.38, bf16[1,768,3072]{2,1,0:T(8,128)(2,1)} %param.23, bf16[8,1,192,768]{3,2,1,0:T(8,128)(2,1)} %all-to-all-done.2), kind=kOutput, calls=%fused_computation.18 | convolution fusion | flops 7342129152 | bytes 35389440 | tf_op jit(solution)/shard_map/nekd,edf->nekf/dot_general | solution.py:158
  250.7 3.6 copy-done.38
  254.3 11.1 %convert_bitcast_fusion = bf16[8,1,192,768]{3,2,1,0:T(8,128)(2,1)} fusion(bf16[1,768,3072]{2,1,0:T(8,128)(2,1)} %param.22, bf16[8,1,192,3072]{3,2,0,1:T(8,128)(2,1)S(1)} %fusion.8), kind=kOutput, calls=%fused_computation.75 | convolution fusion | flops 7248936960 | bytes 16515072 | tf_op jit(solution)/shard_map/nekf,edf->nekd/dot_general | solution.py:164
  265.4 17.9 %all-to-all-done.1 = bf16[8,1,192,768]{3,2,1,0:T(8,128)(2,1)} async-done(((bf16[8,1,192,768]{3,2,1,0:T(8,128)(2,1)}), bf16[8,1,192,768]{3,2,1,0:T(8,128)(2,1)}, u32[]{:S(2)}, u32[]{:S(2)}) %all-to-all-start.1) | async-done | bytes 2359328 | tf_op jit(solution)/shard_map/all_to_all | solution.py:129
  283.3 4.4 all-to-all-start.3
  287.8 3.3 concatenate.10
  291.0 7.7 gather_fusion.1
  298.8 4.9 reshape.522
  303.7 9.4 %multiply_reduce_fusion.1 = (f32[512,2]{1,0:T(8,128)S(1)}, f32[512,768]{1,0:T(8,128)}) fusion(f32[512,2,768]{2,1,0:T(2,128)} %reshape.522, f32[512,768]{1,0:T(8,128)S(1)} %convert_multiply_fusion.4, f32[512,2]{1,0:T(8,128)S(1)} %copy.127), kind=kLoop, calls=%fused_computation.60 | loop fusion | flops 2751488 | bytes 6299648 | tf_op jit(solution)/shard_map/reduce_sum | solution.py:144
  313.4 28.9 %all-to-all-done.3 = bf16[8,1,192,768]{3,2,1,0:T(8,128)(2,1)} async-done(((bf16[8,1,192,768]{3,2,1,0:T(8,128)(2,1)}), bf16[8,1,192,768]{3,2,1,0:T(8,128)(2,1)}, u32[]{:S(2)}, u32[]{:S(2)}) %all-to-all-start.3) | async-done | bytes 2359328 | tf_op jit(solution)/shard_map/all_to_all | solution.py:167
  344.2 5.2 gather_fusion.4
  349.4 5.2 reshape.523
  354.6 5.7 reduce_sum.183
  367.8 7.7 fusion.69
  375.4 7.7 multiply_reduce_fusion
  383.2 5.3 multiply_convert_fusion
  388.5 10.4 %fusion.73 = f32[12,32]{1,0:T(8,128)S(1)} fusion(s32[512,512]{0,1:T(8,128)} %copy-done.12, bf16[12,512,512]{1,2,0:T(8,128)(2,1)} %multiply_convert_fusion), kind=kOutput, calls=%fused_computation.100 | convolution fusion | flops 209715200 | bytes 7341568 | tf_op jit(solution)/shard_map/while/body/eval_jaxpr/hqk,qkb->hb/dot_general | solution.py:221
  398.9 4.9 multiply_convert_fusion.2
  405.2 5.2 fusion.94
  410.4 3.6 fusion.63
  414.0 188.6 %all-reduce.11 = (bf16[768,2304]{1,0:T(8,128)(2,1)}, bf16[768,768]{1,0:T(8,128)(2,1)}, bf16[768,8]{0,1:T(8,128)(2,1)S(1)}, bf16[768]{0:T(1024)(128)(2,1)S(1)}, b...) all-reduce(f32[768,2304]{1,0:T(8,128)} %fusion.94, ...), channel_id=1, replica_groups=mesh['dp'=4,'expert'=8] {'expert'}, use_global_device_ids=true, to_apply=%region_20.21 | all-reduce | flops 2367360 | bytes 14204160 | tf_op jit(solution)/shard_map/psum | solution.py:248
  604.1 14.3 %fusion.43 = bf16[1,768,3072]{2,1,0:T(8,128)(2,1)} fusion(f32[8,192,3072]{2,1,0:T(8,128)} %fusion.38, bf16[8,1,192,768]{3,2,1,0:T(8,128)(2,1)} %all-to-all-done.2), kind=kOutput, calls=%fused_computation.58 | convolution fusion | flops 7292583936 | bytes 25952256 | tf_op jit(solution)/shard_map/nekd,nekf->edf/dot_general | solution.py:160
  618.5 12.5 %fusion.40 = bf16[1,768,3072]{2,1,0:T(8,128)(2,1)} fusion(bf16[8,1,192,3072]{3,2,0,1:T(8,128)(2,1)} %copy-done.38, bf16[8,1,192,768]{3,2,1,0:T(8,128)(2,1)} %all-to-all-done), kind=kOutput, calls=%fused_computation.57 | convolution fusion | flops 7250116608 | bytes 16515072 | tf_op jit(solution)/shard_map/nekd,nekf->edf/dot_general | solution.py:163
  633.1 9.6 %all-reduce.8 = (bf16[768]{0:T(1024)(128)(2,1)S(1)}, bf16[768]{0:T(1024)(128)(2,1)S(1)}, bf16[12,32]{1,0:T(8,128)(2,1)S(1)}) all-reduce(bf16[768]{0:T(1024)(128)(2,1)S(1)} %get-tuple-element.77, bf16[768]{0:T(1024)(128)(2,1)S(1)} %get-tuple-element.78, ...), channel_id=5, replica_groups=mesh['dp'=4,'expert'=8] {'dp'}, use_global_device_ids=true, to_apply=%region_28.29.clone | all-reduce | flops 1920 | bytes 7680
  648.8 8.6 %reduce-scatter.10.cloned.1.call-done = bf16[192,768]{1,0:T(8,128)(2,1)} async-done(((bf16[768,768]{1,0:T(8,128)(2,1)}), bf16[192,768]{1,0:T(8,128)(2,1)}) %reduce-scatter.10.cloned.1.call-update) | async-done | bytes 294928 | tf_op jit(solution)/shard_map/reduce_scatter | solution.py:256
  659.2 58.0 %reduce-scatter.14.cloned.1.call-done = bf16[1,768,768]{2,1,0:T(8,128)(2,1)} async-done(((bf16[1,768,3072]{2,1,0:T(8,128)(2,1)}), bf16[1,768,768]{2,1,0:T(8,128)(2,1)}) %reduce-scatter.14.cloned.1.call-update) | async-done | bytes 1179664 | tf_op jit(solution)/shard_map/reduce_scatter | solution.py:172
  720.1 57.0 %reduce-scatter.12.cloned.1.call-done = bf16[1,768,768]{2,1,0:T(8,128)(2,1)} async-done(((bf16[1,768,3072]{2,1,0:T(8,128)(2,1)}), bf16[1,768,768]{2,1,0:T(8,128)(2,1)}) %reduce-scatter.12.cloned.1.call-update) | async-done | bytes 1179664 | tf_op jit(solution)/shard_map/reduce_scatter | solution.py:169
  779.9 47.4 %reduce-scatter.8.cloned.1.call-done = bf16[192,2304]{1,0:T(8,128)(2,1)} async-done(((bf16[768,2304]{1,0:T(8,128)(2,1)}), bf16[192,2304]{1,0:T(8,128)(2,1)}) %reduce-scatter.8.cloned.1.call-update) | async-done | bytes 884752 | tf_op jit(solution)/shard_map/reduce_scatter | solution.py:253
  (190 shorter events, 55.3 us)
Async XLA Ops:
  7.2 5.5 copy-start.32
  7.2 5.2 copy-start.15
  7.2 6.8 copy-start.36
  7.2 7.0 copy-start.37
  7.2 18.8 %copy-start.33 = (bf16[3,32]{1,0:T(4,128)(2,1)S(1)}, bf16[3,32]{1,0:T(4,128)(2,1)}, u32[]{:S(2)}) copy-start(bf16[3,32]{1,0:T(4,128)(2,1)} %param.21) | copy-start | bytes 580
  7.2 52.6 %all-gather.5.cloned.1.call-start = ((), (), s32[]{:S(2)}) async-start(), calls=%async_computation.9 | async-start | bytes 4423680 | tf_op jit(solution)/shard_map/all_gather | solution.py:38
  8.0 86.6 %all-gather.7.cloned.1.call-start = ((), (), s32[]{:S(2)}) async-start(), calls=%async_computation.10 | async-start | bytes 1474560 | tf_op jit(solution)/shard_map/all_gather | solution.py:39
  12.4 45.4 %copy-start.12 = (s32[512,512]{0,1:T(8,128)}, s32[512,512]{0,1:T(8,128)S(1)}, u32[]{:S(2)}) copy-start(s32[512,512]{0,1:T(8,128)S(1)} %compare_select_fusion) | copy-start | bytes 3145732
  12.7 20.7 %copy-start.23 = (f32[512]{0:T(512)}, f32[512]{0:T(512)S(1)}, u32[]{:S(2)}) copy-start(f32[512]{0:T(512)S(1)} %fusion.67) | copy-start | bytes 6148
  12.7 47.1 %copy-start.29 = (f32[512]{0:T(512)}, f32[512]{0:T(512)S(1)}, u32[]{:S(2)}) copy-start(f32[512]{0:T(512)S(1)} %fusion.115) | copy-start | bytes 6148
  26.0 33.8 %copy-start.25 = (f32[768]{0:T(1024)}, f32[768]{0:T(1024)S(1)}, u32[]{:S(2)}) copy-start(f32[768]{0:T(1024)S(1)} %convert_element_type.378) | copy-start | bytes 9220
  37.0 7.7 copy-start.27
  65.2 17.3 %copy-start.6 = (bf16[512,768]{0,1:T(8,128)(2,1)}, bf16[512,768]{0,1:T(8,128)(2,1)S(1)}, u32[]{:S(2)}) copy-start(bf16[512,768]{0,1:T(8,128)(2,1)S(1)} %copy.123) | copy-start | bytes 2359300
  66.9 15.6 %copy-start.10 = (bf16[512,768]{0,1:T(8,128)(2,1)}, bf16[512,768]{0,1:T(8,128)(2,1)S(1)}, u32[]{:S(2)}) copy-start(bf16[512,768]{0,1:T(8,128)(2,1)S(1)} %copy.122) | copy-start | bytes 2359300
  82.5 4.6 copy-start
  87.4 7.1 copy-start.14
  94.5 3.9 copy-start.20
  105.1 4.8 copy-start.31
  105.1 13.0 %copy-start.17 = (bf16[512,768]{1,0:T(8,128)(2,1)S(1)}, bf16[512,768]{1,0:T(8,128)(2,1)}, u32[]{:S(2)}) copy-start(bf16[512,768]{1,0:T(8,128)(2,1)} %param.13) | copy-start | bytes 2359300
  105.1 59.5 %all-to-all-start = ((bf16[8,1,192,768]{3,2,1,0:T(8,128)(2,1)}), bf16[8,1,192,768]{3,2,1,0:T(8,128)(2,1)}, u32[]{:S(2)}, u32[]{:S(2)}) async-start(bf16[8,1,192,768]{3,2,1,0:T(8,128)(2,1)} %broadcast_multiply_fusion), calls=%async_computation | async-start | bytes 4718592 | tf_op jit(solution)/shard_map/all_to_all | solution.py:123
  118.4 5.9 copy-start.22
  164.6 59.5 %all-to-all-start.2 = ((bf16[8,1,192,768]{3,2,1,0:T(8,128)(2,1)}), bf16[8,1,192,768]{3,2,1,0:T(8,128)(2,1)}, u32[]{:S(2)}, u32[]{:S(2)}) async-start(bf16[8,1,192,768]{3,2,1,0:T(8,128)(2,1)} %multiply_convert_fusion.1), calls=%async_computation.2 | async-start | bytes 4718592 | tf_op jit(solution)/shard_map/all_to_all | solution.py:154
  224.1 59.2 %all-to-all-start.1 = ((bf16[8,1,192,768]{3,2,1,0:T(8,128)(2,1)}), bf16[8,1,192,768]{3,2,1,0:T(8,128)(2,1)}, u32[]{:S(2)}, u32[]{:S(2)}) async-start(bf16[8,1,192,768]{3,2,1,0:T(8,128)(2,1)} %convert_bitcast_fusion.1), calls=%async_computation.1 | async-start | bytes 4718592 | tf_op jit(solution)/shard_map/all_to_all | solution.py:129
  250.7 3.7 copy-start.38
  265.4 22.3 %copy-start.28 = (s32[1024,1]{0,1:T(1,128)S(1)}, s32[1024,1]{0,1:T(1,128)}, u32[]{:S(2)}) copy-start(s32[1024,1]{0,1:T(1,128)} %copy-done.27) | copy-start | bytes 12292
  283.3 59.0 %all-to-all-start.3 = ((bf16[8,1,192,768]{3,2,1,0:T(8,128)(2,1)}), bf16[8,1,192,768]{3,2,1,0:T(8,128)(2,1)}, u32[]{:S(2)}, u32[]{:S(2)}) async-start(bf16[8,1,192,768]{3,2,1,0:T(8,128)(2,1)} %convert_bitcast_fusion), calls=%async_computation.3 | async-start | bytes 4718592 | tf_op jit(solution)/shard_map/all_to_all | solution.py:167
  287.7 359.7 %reduce-scatter.16.cloned.1.call-start = ((), (), s32[]{:S(2)}) async-start(), calls=%async_computation.15 | async-start | bytes 245760
  354.6 5.7 copy-start.5
  360.4 1.4 copy-start.13
  360.4 1.6 copy-start.18
  362.0 1.5 copy-start.21
  363.4 2.3 copy-start.2
  363.4 2.3 copy-start.35
  367.8 15.4 %slice-start = ((s8[12582912]{0:T(1024)(128)(4,1)}), s8[4194304]{0:T(1024)(128)(4,1)S(1)}, s32[]{:S(2)}) async-start(s8[12582912]{0:T(1024)(128)(4,1)} %bitcast.209), calls=%async_computation.16 | async-start | bytes 8388608
  367.8 15.4 %slice-start.1 = ((s8[12582912]{0:T(1024)(128)(4,1)}), s8[4194304]{0:T(1024)(128)(4,1)S(1)}, s32[]{:S(2)}) async-start(s8[12582912]{0:T(1024)(128)(4,1)} %bitcast.209), calls=%async_computation.17 | async-start | bytes 8388608
  375.4 7.8 slice-start.2
  388.5 10.4 %copy-start.11 = (bf16[512,768]{0,1:T(8,128)(2,1)S(1)}, bf16[512,768]{0,1:T(8,128)(2,1)}, u32[]{:S(2)}) copy-start(bf16[512,768]{0,1:T(8,128)(2,1)} %copy-done.10) | copy-start | bytes 2359300
  398.9 5.0 copy-start.1
  398.9 5.0 copy-start.7
  403.9 1.4 copy-start.19
  405.2 5.2 copy-start.34
  410.4 3.6 copy-start.8
  603.5 53.9 %reduce-scatter.10.cloned.1.call-start = ((), (), s32[]{:S(2)}) async-start(), calls=%async_computation.12 | async-start | bytes 1474560 | tf_op jit(solution)/shard_map/reduce_scatter | solution.py:256
  604.1 113.2 %reduce-scatter.14.cloned.1.call-start = ((), (), s32[]{:S(2)}) async-start(), calls=%async_computation.14 | async-start | bytes 5898240 | tf_op jit(solution)/shard_map/reduce_scatter | solution.py:172
  618.5 158.6 %reduce-scatter.12.cloned.1.call-start = ((), (), s32[]{:S(2)}) async-start(), calls=%async_computation.13 | async-start | bytes 5898240 | tf_op jit(solution)/shard_map/reduce_scatter | solution.py:169
  631.0 13.6 %copy-start.24 = (f32[512]{0:T(512)S(1)}, f32[512]{0:T(512)}, u32[]{:S(2)}) copy-start(f32[512]{0:T(512)} %copy-done.23) | copy-start | bytes 6148
  631.0 13.6 %copy-start.3 = (f32[512,768]{1,0:T(8,128)S(1)}, f32[512,768]{1,0:T(8,128)}, u32[]{:S(2)}) copy-start(f32[512,768]{1,0:T(8,128)} %copy-done.2) | copy-start | bytes 4718596
  631.1 196.3 %reduce-scatter.8.cloned.1.call-start = ((), (), s32[]{:S(2)}) async-start(), calls=%async_computation.11 | async-start | bytes 4423680 | tf_op jit(solution)/shard_map/reduce_scatter | solution.py:253
  (5 other events, 5.9 us)
Sparse Core Ops, SparseCore 0:
  9.9 49.8 all-gather.4
  61.6 27.5 all-gather.6
  603.6 21.6 reduce-scatter.15
  628.7 28.6 reduce-scatter.9
  660.3 56.9 reduce-scatter.13
  720.1 56.9 reduce-scatter.11
  780.2 47.1 reduce-scatter.7
where the time goes:
time: 844 us; the launch traced here: 837 us
  waiting for transfers between devices  276 us (33%)
  blocking collectives  225 us (27%)
  matrix products  174 us (21%)
  local copies, waits for them, and re-layouts  75.8 us (9%)
  other arithmetic  49.6 us (6%)
  starting transfers between devices  18.8 us (2%)
  between operations  17.8 us (2%)
    psum x1, blocking collectives, on_device(): lax.psum((grad_qkv, grad_attn_out, grad_router, grad_gain_attn, grad_gain...  189 us
    reduce_scatter x1, waiting for transfers between devices, on_device(): lax.psum_scatter(full_w_out.astype(jnp.bfloat16), 'dp', scatter_dimension...  58 us
    reduce_scatter x1, waiting for transfers between devices, on_device(): lax.psum_scatter(full_w_in.astype(jnp.bfloat16), 'dp', scatter_dimension=...  57 us
    reduce_scatter x1, waiting for transfers between devices, on_device(): lax.psum_scatter(summed[0].astype(jnp.bfloat16), 'dp', scatter_dimension=...  47.4 us
    all_to_all x1, waiting for transfers between devices, on_device(): lax.all_to_all(send_rows, 'expert', split_axis=0, concat_axis=0, tiled=True)  29.9 us
    all_to_all x1, waiting for transfers between devices, on_device(): lax.all_to_all(d_rows, 'expert', split_axis=0, concat_axis=0, tiled=True)  28.9 us
    all_to_all x1, waiting for transfers between devices, on_device(): lax.all_to_all(d_send, 'expert', split_axis=0, concat_axis=0, tiled=True)  23.6 us
    dot_general x1, matrix products, on_device(): jnp.einsum('nekd,edf->nekf', d_recv, w_out, preferred_element_type=jnp.fl...  22 us
  transfers between devices with their start and end apart: 11, of which 9 were waited for; matrix products, arithmetic and copies ran while one was open for 25% of the time, Pallas kernels for 0%

commit v1 on v0

v1 whole, which is shorter than its diff:
```python
import functools
import math

import jax
import jax.numpy as jnp
from jax import lax
from jax.experimental import pallas as pl
from jax.experimental.pallas import tpu as pltpu
from jax.sharding import PartitionSpec as P

norm_eps = 1e-06
rel_edges = (19, 21, 24, 27, 31, 35, 40, 46, 52, 59, 67, 77, 87, 99, 113)
far_start = 113
bf16 = jnp.bfloat16
f32 = jnp.float32
neg_big = -1e30
tile = 128
gelu_c = math.sqrt(2.0 / math.pi)
gelu_k = 0.044715


def bucket_of(distance):
    far_bucket = jnp.full(distance.shape, 16, jnp.int32)
    for edge_value in rel_edges:
        far_bucket = far_bucket + (distance >= edge_value).astype(jnp.int32)
    return jnp.where(distance < 16, distance, far_bucket)


def mm(a, b, ca=1, cb=0):
    return lax.dot_general(a, b, (((ca,), (cb,)), ((), ())), preferred_element_type=f32)


def round_up(a, b):
    return (a + b - 1) // b * b


def head_tiles(rev_ref, hh):
    row = rev_ref[0, hh : hh + 1, :]
    toe = pltpu.roll(jnp.broadcast_to(row, (tile, 2 * tile)), 0, 1, stride=1, stride_axis=0)
    down = lax.broadcasted_iota(jnp.int32, (tile, tile), 0)
    across = lax.broadcasted_iota(jnp.int32, (tile, tile), 1)
    diag = jnp.where(down >= across, toe[:, :tile], neg_big)
    return diag, toe[:, tile:], jnp.broadcast_to(row[:, tile : tile + 1], (tile, tile))


def score_tiles(q_part, k_ref, km_ref, bias, qb, count):
    keys = (qb + 1) * tile
    raw = mm(q_part, k_ref[0:keys, :], 1, 1)
    out = []
    for kb in range(qb + 1):
        part = raw[:, kb * tile : (kb + 1) * tile] + bias[min(qb - kb, 2)]
        if (kb + 1) * tile > 3 * count // 4:
            part = part + km_ref[0:1, kb * tile : (kb + 1) * tile]
        out.append(part)
    return out


def attn_fwd_kernel(q_ref, k_ref, v_ref, rev_ref, km_ref, o_ref, lse_ref):
    count = q_ref.shape[0]
    width = q_ref.shape[1]
    lane = lax.broadcasted_iota(jnp.int32, (1, width), 1)
    first = lane < width // 2
    scale = jnp.asarray((width // 2) ** (-0.5), bf16)
    biases = [head_tiles(rev_ref, hh) for hh in range(2)]
    for qb in range(count // tile):
        rows = slice(qb * tile, (qb + 1) * tile)
        outs, lses = [], []
        for hh in range(2):
            mine = first if hh == 0 else jnp.logical_not(first)
            q_part = jnp.where(mine, q_ref[rows, :] * scale, jnp.zeros((), bf16))
            parts = score_tiles(q_part, k_ref, km_ref, biases[hh], qb, count)
            top = functools.reduce(jnp.maximum, parts)
            top = jnp.max(top, axis=1, keepdims=True)
            exps = [jnp.exp(part - top) for part in parts]
            total = jnp.sum(functools.reduce(jnp.add, exps), axis=1, keepdims=True)
            inv = 1.0 / total
            probs = jnp.concatenate([(e * inv).astype(bf16) for e in exps], axis=1)
            outs.append(mm(probs, v_ref[0 : (qb + 1) * tile, :]))
            lses.append(top + jnp.log(total))
        o_ref[rows, :] = jnp.where(first, outs[0], outs[1]).astype(bf16)
        lse_ref[0, rows, :] = jnp.where(first, lses[0], lses[1])


def attention_forward(qkv, rev, key_mask):
    count, three = qkv.shape
    width = three // 3
    pairs = width // tile
    return pl.pallas_call(
        attn_fwd_kernel,
        grid=(pairs,),
        in_specs=[
            pl.BlockSpec((count, tile), lambda h: (0, h)),
            pl.BlockSpec((count, tile), lambda h: (0, h + pairs)),
            pl.BlockSpec((count, tile), lambda h: (0, h + 2 * pairs)),
            pl.BlockSpec((1, 2, 2 * tile), lambda h: (h, 0, 0)),
            pl.BlockSpec((1, count), lambda h: (0, 0)),
        ],
        out_specs=[
            pl.BlockSpec((count, tile), lambda h: (0, h)),
            pl.BlockSpec((1, count, tile), lambda h: (h, 0, 0)),
        ],
        out_shape=[
            jax.ShapeDtypeStruct((count, width), bf16),
            jax.ShapeDtypeStruct((pairs, count, tile), f32),
        ],
        cost_estimate=pl.CostEstimate(
            flops=4 * count * count * width, bytes_accessed=16 * count * width, transcendentals=0
        ),
        name="attn_fwd",
    )(qkv, qkv, qkv, rev, key_mask)


def unskew(block):
    down = lax.broadcasted_iota(jnp.int32, block.shape, 0)
    lanes = block.shape[1]
    step = 1
    while step < block.shape[0]:
        moved = pltpu.roll(block, lanes - step, 1)
        block = jnp.where((down & step) != 0, moved, block)
        step *= 2
    return block


def attn_bwd_kernel(
    q_ref, k_ref, v_ref, do_ref, lse_ref, rev_ref, km_ref, dq_ref, dk_ref, dv_ref, db_ref, dk_acc, dv_acc
):
    count = q_ref.shape[0]
    width = q_ref.shape[1]
    lane = lax.broadcasted_iota(jnp.int32, (1, width), 1)
    first = lane < width // 2
    scale = (width // 2) ** (-0.5)
    zero = jnp.zeros((), bf16)
    biases = [head_tiles(rev_ref, hh) for hh in range(2)]
    near = [[None, None, None] for _ in range(2)]
    for qb in reversed(range(count // tile)):
        rows = slice(qb * tile, (qb + 1) * tile)
        keys = (qb + 1) * tile
        dq, dk, dv = 0.0, 0.0, 0.0
        for hh in range(2):
            mine = first if hh == 0 else jnp.logical_not(first)
            q_part = jnp.where(mine, q_ref[rows, :] * jnp.asarray(scale, bf16), zero)
            do_part = jnp.where(mine, do_ref[rows, :], zero)
            lse = lse_ref[0, rows, hh * (width // 2) : hh * (width // 2) + 1]
            parts = score_tiles(q_part, k_ref, km_ref, biases[hh], qb, count)
            dp = mm(do_part, v_ref[0:keys, :], 1, 1)
            probs = [jnp.exp(part - lse) for part in parts]
            dps = [dp[:, kb * tile : (kb + 1) * tile] for kb in range(qb + 1)]
            prods = [p * d for p, d in zip(probs, dps)]
            mean = jnp.sum(functools.reduce(jnp.add, prods), axis=1, keepdims=True)
            ds = [(p * (d - mean)).astype(bf16) for p, d in zip(probs, dps)]
            for kb in range(qb + 1):
                gap = min(qb - kb, 2)
                wide = ds[kb].astype(f32)
                near[hh][gap] = wide if near[hh][gap] is None else near[hh][gap] + wide
            ds_all = jnp.concatenate(ds, axis=1)
            p_all = jnp.concatenate([p.astype(bf16) for p in probs], axis=1)
            k_part = jnp.where(mine, k_ref[0:keys, :], zero)
            dq = dq + mm(ds_all, k_part)
            dk = dk + mm(ds_all, q_part, 0, 0)
            dv = dv + mm(p_all, do_part, 0, 0)
        dq_ref[rows, :] = (dq * scale).astype(bf16)
        if keys == count:
            dk_acc[...] = dk
            dv_acc[...] = dv
        else:
            dk_acc[0:keys, :] += dk
            dv_acc[0:keys, :] += dv
    dk_ref[...] = dk_acc[...].astype(bf16)
    dv_ref[...] = dv_acc[...].astype(bf16)
    for hh in range(2):
        diag, below, far = near[hh]
        if below is None:
            below = jnp.zeros_like(diag)
        line = jnp.sum(unskew(jnp.concatenate([diag, below], axis=1)), axis=0, keepdims=True)
        if far is not None:
            total = jnp.sum(far)
            spot = lax.broadcasted_iota(jnp.int32, line.shape, 1) == tile
            line = line + jnp.where(spot, total, 0.0)
        db_ref[0, hh : hh + 1, :] = line


def attention_backward(qkv, d_attn, lse, rev, key_mask):
    count, three = qkv.shape
    width = three // 3
    pairs = width // tile
    block = pl.BlockSpec((count, tile), lambda h: (0, h))
    return pl.pallas_call(
        attn_bwd_kernel,
        grid=(pairs,),
        in_specs=[
            block,
            pl.BlockSpec((count, tile), lambda h: (0, h + pairs)),
            pl.BlockSpec((count, tile), lambda h: (0, h + 2 * pairs)),
            block,
            pl.BlockSpec((1, count, tile), lambda h: (h, 0, 0)),
            pl.BlockSpec((1, 2, 2 * tile), lambda h: (h, 0, 0)),
            pl.BlockSpec((1, count), lambda h: (0, 0)),
        ],
        out_specs=[block, block, block, pl.BlockSpec((1, 2, 2 * tile), lambda h: (h, 0, 0))],
        out_shape=[jax.ShapeDtypeStruct((count, width), bf16)] * 3
        + [jax.ShapeDtypeStruct((pairs, 2, 2 * tile), f32)],
        scratch_shapes=[pltpu.VMEM((count, tile), f32), pltpu.VMEM((count, tile), f32)],
        cost_estimate=pl.CostEstimate(
            flops=10 * count * count * width, bytes_accessed=20 * count * width, transcendentals=0
        ),
        name="attn_bwd",
    )(qkv, qkv, qkv, d_attn, lse, rev, key_mask)


def expert_kernel(
    own_ref, x_ref, g_ref, other_ref, win_ref, wout_ref, wr_ref,
    made_ref, drow_ref, act_ref, dpre_ref, dmade_ref, sel_ref, made_acc, drow_acc,
):
    ff = win_ref.shape[1]
    step = 1024
    experts = wr_ref.shape[1] // 2
    x = x_ref[...]
    g = g_ref[...]
    rows = x.shape[0]
    logits = mm(x, wr_ref[...])
    ids = lax.broadcasted_iota(jnp.int32, logits.shape, 1)
    own = own_ref[0]
    other = other_ref[...]
    hit_own = ids == own
    hit_other = ids == other
    diff = jnp.sum(jnp.where(hit_other, logits, 0.0) - jnp.where(hit_own, logits, 0.0), axis=1, keepdims=True)
    pair_own = 1.0 / (1.0 + jnp.exp(diff))
    pair_other = 1.0 / (1.0 + jnp.exp(-diff))
    g_wide = g.astype(f32)
    d_made = (pair_own * g_wide).astype(bf16)
    dmade_ref[...] = d_made

    def body(i, carry):
        cols = pl.ds(pl.multiple_of(i * step, step), step)
        u = mm(x, win_ref[:, cols])
        da = mm(d_made, wout_ref[:, cols])
        u2 = u * u
        h = 0.5 + 0.5 * jnp.tanh(u * (gelu_c + (gelu_c * gelu_k) * u2))
        act = (u * h).astype(bf16)
        slope = h + u * (2.0 * gelu_c + (6.0 * gelu_c * gelu_k) * u2) * (h - h * h)
        dpre = (da * slope).astype(bf16)
        act_ref[:, cols] = act
        dpre_ref[:, cols] = dpre
        m = mm(act, wout_ref[:, cols], 1, 1)
        d = mm(dpre, win_ref[:, cols], 1, 1)

        @pl.when(i == 0)
        def _():
            made_acc[...] = m
            drow_acc[...] = d

        @pl.when(i > 0)
        def _():
            made_acc[...] += m
            drow_acc[...] += d

        return carry

    lax.fori_loop(0, ff // step, body, 0)
    made = made_acc[...].astype(bf16).astype(f32)
    made_ref[...] = (pair_own * made).astype(bf16)
    d_gate = jnp.sum(g_wide * made, axis=1, keepdims=True)
    push = pair_own * pair_other * d_gate
    full = jnp.where(hit_own, push, 0.0) - jnp.where(hit_other, push, 0.0)
    coarse = full.astype(bf16)
    fine = (full - coarse.astype(f32)).astype(bf16)
    lanes = wr_ref.shape[1]
    fine_moved = pltpu.roll(fine.astype(f32), lanes // 2, 1)
    sel = coarse.astype(f32) + fine_moved
    sel = sel.astype(bf16)
    sel_ref[...] = sel
    back = mm(coarse, wr_ref[...], 1, 1)
    drow_ref[...] = (drow_acc[...] + back).astype(bf16)


def expert_pass(own, x_rows, g_rows, other, w_in, w_out, w_router):
    rows, width = x_rows.shape
    ff = w_in.shape[1]
    rt = 256
    lanes = w_router.shape[1]
    row_block = pl.BlockSpec((rt, width), lambda r: (r, 0))
    ff_block = pl.BlockSpec((rt, ff), lambda r: (r, 0))
    once = dict(pipeline_mode=pl.Buffered(1))
    return pl.pallas_call(
        expert_kernel,
        grid=(rows // rt,),
        in_specs=[
            pl.BlockSpec(memory_space=pltpu.SMEM),
            row_block,
            row_block,
            pl.BlockSpec((rt, 1), lambda r: (r, 0)),
            pl.BlockSpec((width, ff), lambda r: (0, 0), **once),
            pl.BlockSpec((width, ff), lambda r: (0, 0), **once),
            pl.BlockSpec((width, lanes), lambda r: (0, 0), **once),
        ],
        out_specs=[row_block, row_block, ff_block, ff_block, row_block, pl.BlockSpec((rt, lanes), lambda r: (r, 0))],
        out_shape=[
            jax.ShapeDtypeStruct((rows, width), bf16),
            jax.ShapeDtypeStruct((rows, width), bf16),
            jax.ShapeDtypeStruct((rows, ff), bf16),
            jax.ShapeDtypeStruct((rows, ff), bf16),
            jax.ShapeDtypeStruct((rows, width), bf16),
            jax.ShapeDtypeStruct((rows, lanes), bf16),
        ],
        scratch_shapes=[pltpu.VMEM((rt, width), f32), pltpu.VMEM((rt, width), f32)],
        compiler_params=pltpu.CompilerParams(vmem_limit_bytes=56 << 20),
        cost_estimate=pl.CostEstimate(
            flops=8 * rows * width * ff, bytes_accessed=4 * rows * ff + 4 * width * ff, transcendentals=0
        ),
        name="expert_pass",
    )(own, x_rows, g_rows, other, w_in, w_out, w_router)


def weight_grad_kernel(x_ref, dm_ref, act_ref, dpre_ref, gin_ref, gout_ref):
    gout_ref[...] = mm(dm_ref[...], act_ref[...], 0, 0).astype(bf16)
    gin_ref[...] = mm(x_ref[...], dpre_ref[...], 0, 0).astype(bf16)


def weight_grads(x_rows, d_made, act, d_pre):
    rows, width = x_rows.shape
    ff = act.shape[1]
    ft = 512
    full = pl.BlockSpec((rows, width), lambda f: (0, 0), pipeline_mode=pl.Buffered(1))
    cols = pl.BlockSpec((rows, ft), lambda f: (0, f))
    outs = pl.BlockSpec((width, ft), lambda f: (0, f))
    return pl.pallas_call(
        weight_grad_kernel,
        grid=(ff // ft,),
        in_specs=[full, full, cols, cols],
        out_specs=[outs, outs],
        out_shape=[jax.ShapeDtypeStruct((width, ff), bf16)] * 2,
        compiler_params=pltpu.CompilerParams(vmem_limit_bytes=56 << 20),
        cost_estimate=pl.CostEstimate(
            flops=4 * rows * width * ff, bytes_accessed=4 * rows * ff + 4 * width * ff, transcendentals=0
        ),
        name="weight_grads",
    )(x_rows, d_made, act, d_pre)


def rms_scale(vector):
    return lax.rsqrt(jnp.mean(vector * vector, axis=-1, keepdims=True) + norm_eps)


def rms_back(vector, scale, gain_vec, cotangent):
    inner = cotangent * gain_vec
    push = jnp.mean(inner * vector, axis=-1, keepdims=True)
    d_vector = scale * inner - vector * (scale * scale * scale) * push
    d_gain = jnp.sum(cotangent * (vector * scale), axis=0)
    return d_vector, d_gain


def on_device(
    inputs, cotangent, lengths, routes, w_qkv, w_attn_out, w_router,
    gain_attn, gain_moe, rel_bias, w_in, w_out,
):
    tok_count, model_width = inputs.shape
    group = lax.axis_size("expert")
    dp_count = lax.axis_size("dp")
    shard = w_qkv.shape[0]
    head_count = rel_bias.shape[0] * dp_count
    bucket_count = rel_bias.shape[1]
    expert_count = w_router.shape[1]
    assert w_in.shape[0] == 1 and expert_count == group and routes.shape[1] == 2
    capacity = round_up(3 * tok_count * 2 // (2 * expert_count), 32)
    rows = expert_count * capacity

    bias_cells = rel_bias.size
    small = jnp.concatenate(
        [
            w_router,
            gain_attn[:, None],
            gain_moe[:, None],
            jnp.pad(rel_bias.reshape(-1), (0, shard - bias_cells))[:, None],
        ],
        axis=1,
    )
    small = jnp.pad(small, ((0, 0), (0, tile - small.shape[1])))
    gathered = lax.all_gather(jnp.concatenate([w_qkv, small], axis=1), "dp", axis=0, tiled=True)
    w_mix = lax.all_gather(w_attn_out, "dp", axis=0, tiled=True)
    w_proj = gathered[:, : 3 * model_width]
    small_all = gathered[:, 3 * model_width :]
    w_gate = small_all[:, :expert_count]
    gain_first = small_all[:, expert_count].astype(f32)
    gain_second = small_all[:, expert_count + 1].astype(f32)
    bias_table = small_all[:, expert_count + 2].reshape(dp_count, shard)[:, :bias_cells]
    bias_table = bias_table.reshape(head_count, bucket_count)

    positions = jnp.arange(tok_count, dtype=jnp.int32)
    valid = positions < lengths[0]
    valid_mask = valid.astype(f32)[:, None]
    expert_ids = jnp.arange(expert_count, dtype=jnp.int32)
    hot = jnp.any(routes[:, :, None] == expert_ids, axis=1) & valid[:, None]
    hot_b = hot.astype(bf16)
    lower = (positions[:, None] > positions[None, :]).astype(bf16)
    rank = jnp.dot(lower, hot_b, preferred_element_type=f32).astype(jnp.int32)
    rank = jnp.where(hot, rank, -1)
    slots = jnp.arange(capacity, dtype=jnp.int32)
    select = (rank.T[:, None, :] == slots[None, :, None]).astype(bf16).reshape(rows, tok_count)
    both = jnp.sum(routes, axis=1)
    other_tok = (both[:, None] - expert_ids[None, :]) * hot.astype(jnp.int32) - (1 - hot.astype(jnp.int32))
    chosen = rank.T[:, None, :] == slots[None, :, None]
    other_slot = jnp.sum(jnp.where(chosen, both[None, None, :], 0), axis=2) - expert_ids[:, None]

    def to_experts(block):
        return lax.all_to_all(
            block.reshape((group, capacity) + block.shape[1:]), "expert", split_axis=0, concat_axis=0, tiled=True
        ).reshape(block.shape)

    g_rows = to_experts(jnp.dot(select, cotangent, preferred_element_type=f32).astype(bf16))
    other = to_experts(other_slot.reshape(rows, 1))

    distances = (2 * tile - jnp.arange(2 * tile, dtype=jnp.int32)) % (2 * tile)
    bucket_hot = (bucket_of(distances)[:, None] == jnp.arange(bucket_count)).astype(f32)
    rev = jnp.sum(bias_table.astype(f32)[:, None, :] * bucket_hot[None], axis=-1)
    rev = rev.reshape(head_count // 2, 2, 2 * tile)
    key_mask = jnp.where(valid, 0.0, neg_big)[None, :].astype(f32)
    inputs_wide = inputs.astype(f32)
    scale_first = rms_scale(inputs_wide)
    normed_attn = (inputs_wide * scale_first * gain_first).astype(bf16)
    qkv = jnp.dot(normed_attn, w_proj, preferred_element_type=f32).astype(bf16)
    attn_heads, lse = attention_forward(qkv, rev, key_mask)
    hidden = inputs_wide + valid_mask * jnp.dot(attn_heads, w_mix, preferred_element_type=f32)
    scale_second = rms_scale(hidden)
    normed_moe = (hidden * scale_second * gain_second).astype(bf16)

    x_rows = to_experts(jnp.dot(select, normed_moe, preferred_element_type=f32).astype(bf16))
    lanes = max(tile, 2 * expert_count)
    w_gate_wide = jnp.zeros((model_width, lanes), bf16).at[:, :expert_count].set(w_gate)
    own = lax.axis_index("expert").astype(jnp.int32).reshape(1)
    made, d_rows, act, d_pre, d_made, sel = expert_pass(
        own, x_rows, g_rows, other, w_in[0], w_out[0], w_gate_wide
    )
    d_back = to_experts(d_rows)
    made_back = to_experts(made)
    full_in, full_out = weight_grads(x_rows, d_made, act, d_pre)
    grad_w_in = lax.psum_scatter(full_in, "dp", scatter_dimension=1, tiled=True).astype(f32)[None]
    grad_w_out = lax.psum_scatter(full_out, "dp", scatter_dimension=1, tiled=True).astype(f32)[None]
    router_wide = jnp.dot(x_rows.T, sel, preferred_element_type=f32)
    grad_router = router_wide[:, :expert_count] + router_wide[:, lanes // 2 : lanes // 2 + expert_count]

    moe_out = jnp.dot(select.T, made_back, preferred_element_type=f32)
    outputs = (valid_mask * (hidden + moe_out)).astype(bf16)

    d_normed = jnp.dot(select.T, d_back, preferred_element_type=f32)
    d_hidden_norm, grad_gain_moe = rms_back(hidden, scale_second, gain_second, d_normed)
    d_hidden = cotangent.astype(f32) * valid_mask + d_hidden_norm
    d_proj = (d_hidden * valid_mask).astype(bf16)
    grad_attn_out = jnp.dot(attn_heads.T, d_proj, preferred_element_type=f32)
    d_heads = jnp.dot(d_proj, w_mix.T, preferred_element_type=f32).astype(bf16)
    dq, dk, dv, d_line = attention_backward(qkv, d_heads, lse, rev, key_mask)
    d_qkv = jnp.concatenate([dq, dk, dv], axis=1)
    near = jnp.arange(2 * tile, dtype=jnp.int32)
    line_hot = (bucket_of((2 * tile - near) % (2 * tile))[:, None] == jnp.arange(bucket_count)).astype(f32)
    grad_rel_bias = jnp.sum(d_line.reshape(head_count, 2 * tile, 1) * line_hot[None], axis=1)
    grad_qkv = jnp.dot(normed_attn.T, d_qkv, preferred_element_type=f32)
    d_normed_attn = jnp.dot(d_qkv, w_proj.T, preferred_element_type=f32)
    d_norm_in, grad_gain_attn = rms_back(inputs_wide, scale_first, gain_first, d_normed_attn)
    d_inputs = (d_hidden + d_norm_in).astype(bf16)

    bias_col = jnp.pad(
        grad_rel_bias.reshape(dp_count, bias_cells), ((0, 0), (0, shard - bias_cells))
    ).reshape(model_width, 1)
    small_grad = jnp.concatenate(
        [grad_router, grad_gain_attn[:, None], grad_gain_moe[:, None], bias_col], axis=1
    )
    small_grad = jnp.pad(small_grad, ((0, 0), (0, tile - small_grad.shape[1])))
    packed = jnp.concatenate([grad_qkv, grad_attn_out, small_grad], axis=1).astype(bf16)
    part = lax.psum_scatter(packed, "dp", scatter_dimension=0, tiled=True)
    whole = lax.psum(part, "expert").astype(f32)
    end = 4 * model_width
    tail = whole[:, end:]
    return (
        outputs,
        d_inputs,
        whole[:, : 3 * model_width],
        whole[:, 3 * model_width : end],
        tail[:, :expert_count],
        tail[:, expert_count],
        tail[:, expert_count + 1],
        tail[:bias_cells, expert_count + 2].reshape(rel_bias.shape),
        grad_w_in,
        grad_w_out,
    )


def solution(mesh):
    placed = (
        P(("dp", "expert"), None),
        P(("dp", "expert"), None),
        P(("dp", "expert")),
        P(("dp", "expert"), None),
        P("dp", None),
        P("dp", None),
        P("dp", None),
        P("dp"),
        P("dp"),
        P("dp", None),
        P("expert", None, None),
        P("expert", None, None),
    )
    return jax.shard_map(
        on_device,
        mesh=mesh,
        in_specs=placed,
        out_specs=(
            P(("dp", "expert"), None),
            P(("dp", "expert"), None),
            P("dp", None),
            P("dp", None),
            P("dp", None),
            P("dp"),
            P("dp"),
            P("dp", None),
            P("expert", None, "dp"),
            P("expert", None, "dp"),
        ),
        check_vma=False,
    )
```

time: 844 us -> 572 us (0.68)
  blocking collectives: 225 us -> 0 us
  matrix products: 174 us -> 33.6 us
  Pallas kernels: 0 us -> 103 us
  waiting for transfers between devices: 276 us -> 339 us
  local copies, waits for them, and re-layouts: 75.8 us -> 25.9 us
  other arithmetic: 49.6 us -> 28.5 us
    psum x1 -> x0, blocking collectives: 189 us -> none  [on_device(): lax.psum((grad_qkv, grad_attn_out, grad_router, grad_gain_attn, grad_gain...]
    dot_general x23 -> x12, matrix products: 174 us -> 33.6 us  [the longest x1 5.5 us: on_device(): qkv = jnp.dot(normed_attn, w_proj, preferred_element_type=f32).astype(bf16)]
    pallas_call x0 -> x4, Pallas kernels: none -> 103 us  [the longest x1 47.1 us: expert_pass(): pl.pallas_call(expert_kernel, grid=(rows // rt,), in_specs=[pl.BlockSpec(...]
    reduce_scatter x4 -> x3, waiting for transfers between devices: 171 us -> 88.5 us  [the longest x1 57 us: on_device(): lax.psum_scatter(full_in, 'dp', scatter_dimension=1, tiled=True).astype(f32)]
    psum x0 -> x1, waiting for transfers between devices: none -> 59.4 us  [on_device(): whole = lax.psum(part, 'expert').astype(f32)]
    all_to_all x4 -> x5, waiting for transfers between devices: 100 us -> 157 us  [to_experts(): lax.all_to_all(block.reshape((group, capacity) + block.shape[1:]), 'exper...]
    all_gather x2, waiting for transfers between devices: 2.04 us -> 33.4 us  [the longest x1 31.7 us: on_device(): lax.all_gather(jnp.concatenate([w_qkv, small], axis=1), 'dp', axis=0, til...]
    gather x6 -> x0, local copies, waits for them, and re-layouts: 29.4 us -> none  [the longest x1 7.75 us: on_device(): out_table[slot_index].reshape(tok_count, top_count, model_width)]
  transfers between devices with their start and end apart: 11 -> 11, of which waited for: 9 -> 9; matrix products, arithmetic and copies ran while one was open for 25% -> 7% of each run, Pallas kernels for 0% -> 7%
where the time goes in v1:
time: 572 us; the launch traced here: 570 us
  waiting for transfers between devices  339 us (59%)
  Pallas kernels  103 us (18%)
  matrix products  33.6 us (6%)
  other arithmetic  28.5 us (5%)
  local copies, waits for them, and re-layouts  25.9 us (5%)
  starting transfers between devices  24.5 us (4%)
  between operations  15.2 us (3%)
    all_to_all x5, waiting for transfers between devices, to_experts(): lax.all_to_all(block.reshape((group, capacity) + block.shape[1:]), 'exper...  157 us
    psum x1, waiting for transfers between devices, on_device(): whole = lax.psum(part, 'expert').astype(f32)  59.4 us
    reduce_scatter x1, waiting for transfers between devices, on_device(): lax.psum_scatter(full_in, 'dp', scatter_dimension=1, tiled=True).astype(f32)  57 us
    pallas_call x1, Pallas kernels, expert_pass(): pl.pallas_call(expert_kernel, grid=(rows // rt,), in_specs=[pl.BlockSpec(...  47.1 us
    all_gather x1, waiting for transfers between devices, on_device(): lax.all_gather(jnp.concatenate([w_qkv, small], axis=1), 'dp', axis=0, til...  31.7 us
    reduce_scatter x1, waiting for transfers between devices, on_device(): lax.psum_scatter(full_out, 'dp', scatter_dimension=1, tiled=True)  31.5 us
    all_to_all x5, starting transfers between devices, to_experts(): lax.all_to_all(block.reshape((group, capacity) + block.shape[1:]), 'exper...  24 us
    pallas_call x1, Pallas kernels, weight_grads(): pl.pallas_call(weight_grad_kernel, grid=(ff // ft,), in_specs=[full, full...  20.3 us
  transfers between devices with their start and end apart: 11, of which 9 were waited for; matrix products, arithmetic and copies ran while one was open for 7% of the time, Pallas kernels for 7%

profile of v1, /device:TPU:0, one launch (start us, length us, event | category | flops | bytes accessed | tf_op | source)
XLA Modules:
  0.0 570.1 jit_solution(2473780537661904038)
XLA Ops:
  10.2 2.2 fusion.24
  14.4 6.4 %all-to-all-start.2 = ((s32[8,192,1]{1,2,0:T(1,128)}), s32[8,192,1]{1,2,0:T(1,128)S(1)}, u32[]{:S(2)}, u32[]{:S(2)}) async-start(s32[8,192,1]{1,2,0:T(1,128)} %iota_subtract_fusion), calls=%async_computation.2 | async-start | bytes 16384 | tf_op jit(solution)/shard_map/all_to_all | solution.py:405
  22.2 2.8 convolution_convert_fusion.2
  25.0 1.3 all-to-all-done.2
  26.4 3.9 all-to-all-start.1
  32.4 31.7 %all-gather.3.cloned.1.call-done = bf16[768,2432]{1,0:T(8,128)(2,1)} async-done(((bf16[192,2432]{1,0:T(8,128)(2,1)}), bf16[768,2432]{1,0:T(8,128)(2,1)}) %all-gather.3.cloned.1.call-update) | async-done | bytes 3735568 | tf_op jit(solution)/shard_map/all_gather | solution.py:378
  64.1 1.1 slice_reduce_fusion
  66.2 1.3 convert_reduce_fusion
  67.6 5.5 convolution_convert_fusion.1.q_ref.k_ref.v_ref
  73.1 18.8 %attn_fwd.1 = (bf16[512,768]{1,0:T(8,128)(2,1)}, f32[6,512,128]{2,1,0:T(8,128)}) custom-call(bf16[512,2304]{1,0:T(8,128)(2,1)} %convolution_convert_fusion.1.q_ref.k_ref.v_ref, bf16[512,2304]{1,0:T(8,128)(2,1)} %convolution_convert_fusion.1.q_ref.k_ref.v_ref, bf16[512,2304]{1,0:T(8,128)(2,1)} %convolution_convert_fusion.1.q_ref.k_ref.v_ref, ...), custom_call_target="tpu_custom_call" | custom-call | flops 805306368 | bytes 6291456 | tf_op jit(solution)/shard_map/attn_fwd/pallas_call | solution.py:88
  91.9 1.7 all-gather.5.cloned.1.call-done
  93.6 2.5 multiply_reduce_fusion.1
  97.2 2.9 convolution_convert_fusion.3
  100.2 1.5 copy-done.4
  101.7 4.6 all-to-all-start
  106.9 1.5 reshape.284.other_ref
  108.4 1.6 slice_select_fusion
  110.7 50.2 %all-to-all-done = bf16[8,192,768]{2,1,0:T(8,128)(2,1)S(1)} async-done(((bf16[8,192,768]{2,1,0:T(8,128)(2,1)}), bf16[8,192,768]{2,1,0:T(8,128)(2,1)S(1)}, u32[]{:S(2)}, u32[]{:S(2)}) %all-to-all-start) | async-done | bytes 2359328 | tf_op jit(solution)/shard_map/all_to_all | solution.py:405
  160.9 1.4 copy-done
  162.3 47.1 %expert_pass.1 = (bf16[1536,768]{1,0:T(8,128)(2,1)}, bf16[1536,768]{1,0:T(8,128)(2,1)}, bf16[1536,3072]{1,0:T(8,128)(2,1)}, bf16[1536,3072]{1,0:T(8,128)(2,1)}, ...) custom-call(s32[1]{0:T(128)} %bitcast.2.own_ref, bf16[1536,768]{1,0:T(8,128)(2,1)} %bitcast.50, ...), custom_call_target="tpu_custom_call" | custom-call | flops 28991029248 | bytes 28311552 | tf_op jit(solution)/shard_map/expert_pass/pallas_call | solution.py:284
  209.4 4.7 all-to-all-start.4
  215.3 53.4 %all-to-all-done.4 = bf16[8,192,768]{2,1,0:T(8,128)(2,1)} async-done(((bf16[8,192,768]{2,1,0:T(8,128)(2,1)}), bf16[8,192,768]{2,1,0:T(8,128)(2,1)}, u32[]{:S(2)}, u32[]{:S(2)}) %all-to-all-start.4) | async-done | bytes 2359328 | tf_op jit(solution)/shard_map/all_to_all | solution.py:405
  268.8 4.1 fusion.18
  274.7 0.9 convolution_convert_fusion.4
  276.0 1.7 convolution_convert_fusion.5.do_ref
  277.7 16.9 %attn_bwd.1 = (bf16[512,768]{1,0:T(8,128)(2,1)}, bf16[512,768]{1,0:T(8,128)(2,1)}, bf16[512,768]{1,0:T(8,128)(2,1)}, f32[6,2,256]{2,1,0:T(2,128)}) custom-call(bf16[512,2304]{1,0:T(8,128)(2,1)} %convolution_convert_fusion.1.q_ref.k_ref.v_ref, bf16[512,2304]{1,0:T(8,128)(2,1)} %convolution_convert_fusion.1.q_ref.k_ref.v_ref, ...), custom_call_target="tpu_custom_call" | custom-call | flops 2013265920 | bytes 7864320 | tf_op jit(solution)/shard_map/attn_bwd/pallas_call | solution.py:187
  294.6 1.3 mul.238
  295.9 1.5 multiply_reduce_fusion.2
  297.4 1.3 reshape.275
  298.8 1.3 pad.23
  300.0 1.3 reshape.276
  301.4 1.3 constant_dynamic-update-slice_fusion.2
  303.5 4.0 convolution_convert_fusion
  307.5 3.9 fusion.11
  312.0 1.6 copy.50
  313.5 5.0 fusion.1
  318.8 20.3 %weight_grads.1 = (bf16[768,3072]{1,0:T(8,128)(2,1)}, bf16[768,3072]{1,0:T(8,128)(2,1)}) custom-call(bf16[1536,768]{1,0:T(8,128)(2,1)} %bitcast.51, bf16[1536,768]{1,0:T(8,128)(2,1)} %get-tuple-element.45.dm_ref, bf16[1536,3072]{1,0:T(8,128)(2,1)} %get-tuple-element.46.act_ref, bf16[1536,3072]{1,0:T(8,128)(2,1)} %get-tuple-element.47.dpre_ref), custom_call_target="tpu_custom_call" | custom-call | flops 14495514624 | bytes 28311552 | tf_op jit(solution)/shard_map/weight_grads/pallas_call | solution.py:326
  339.8 4.5 all-to-all-start.3
  344.4 2.7 fusion.16
  347.1 51.8 %all-to-all-done.3 = bf16[8,192,768]{2,1,0:T(8,128)(2,1)} async-done(((bf16[8,192,768]{2,1,0:T(8,128)(2,1)}), bf16[8,192,768]{2,1,0:T(8,128)(2,1)}, u32[]{:S(2)}, u32[]{:S(2)}) %all-to-all-start.3) | async-done | bytes 2359328 | tf_op jit(solution)/shard_map/all_to_all | solution.py:405
  399.0 4.6 fusion.20
  403.6 31.5 %reduce-scatter.8.cloned.1.call-done = bf16[768,768]{1,0:T(8,128)(2,1)} async-done(((bf16[768,3072]{1,0:T(8,128)(2,1)}), bf16[768,768]{1,0:T(8,128)(2,1)}) %reduce-scatter.8.cloned.1.call-update) | async-done | bytes 1179664 | tf_op jit(solution)/shard_map/reduce_scatter | solution.py:437
  435.1 2.8 bitcast_convert_fusion
  438.0 57.0 %reduce-scatter.6.cloned.1.call-done = bf16[768,768]{1,0:T(8,128)(2,1)} async-done(((bf16[768,3072]{1,0:T(8,128)(2,1)}), bf16[768,768]{1,0:T(8,128)(2,1)}) %reduce-scatter.6.cloned.1.call-update) | async-done | bytes 1179664 | tf_op jit(solution)/shard_map/reduce_scatter | solution.py:436
  495.0 2.8 bitcast_convert_fusion.1
  497.8 59.4 %all-reduce.7.cloned.1.call-done = bf16[192,3200]{1,0:T(8,128)(2,1)} async-done(((bf16[192,3200]{1,0:T(8,128)(2,1)}), bf16[192,3200]{1,0:T(8,128)(2,1)}) %all-reduce.7.cloned.1.call-update) | async-done | bytes 1228816 | tf_op jit(solution)/shard_map/psum | solution.py:469
  557.2 1.5 convert_element_type.286
  562.0 1.3 slice.90
  (136 shorter events, 20.2 us)
Async XLA Ops:
  7.2 5.9 %copy-start.24 = (s32[512,2]{0,1:T(2,128)S(1)}, s32[512,2]{0,1:T(2,128)}, u32[]{:S(2)}) copy-start(s32[512,2]{0,1:T(2,128)} %param.17) | copy-start | bytes 12292
  7.2 56.9 %all-gather.3.cloned.1.call-start = ((), (), s32[]{:S(2)}) async-start(), calls=%async_computation.8 | async-start | bytes 4669440 | tf_op jit(solution)/shard_map/all_gather | solution.py:378
  10.2 12.1 %copy-start.7 = (bf16[512,768]{1,0:T(8,128)(2,1)S(1)}, bf16[512,768]{1,0:T(8,128)(2,1)}, u32[]{:S(2)}) copy-start(bf16[512,768]{1,0:T(8,128)(2,1)} %param.15) | copy-start | bytes 2359300
  13.1 80.5 %copy-start.18 = (f32[512]{0:T(512)}, f32[512]{0:T(512)S(1)}, u32[]{:S(2)}) copy-start(f32[512]{0:T(512)S(1)} %get-tuple-element.107) | copy-start | bytes 6148
  14.4 12.0 %all-to-all-start.2 = ((s32[8,192,1]{1,2,0:T(1,128)}), s32[8,192,1]{1,2,0:T(1,128)S(1)}, u32[]{:S(2)}, u32[]{:S(2)}) async-start(s32[8,192,1]{1,2,0:T(1,128)} %iota_subtract_fusion), calls=%async_computation.2 | async-start | bytes 16384 | tf_op jit(solution)/shard_map/all_to_all | solution.py:405
  21.4 0.9 copy-start.9
  26.4 5.2 copy-start.3
  26.4 73.8 %all-to-all-start.1 = ((bf16[8,192,768]{2,1,0:T(8,128)(2,1)}), bf16[8,192,768]{2,1,0:T(8,128)(2,1)S(1)}, u32[]{:S(2)}, u32[]{:S(2)}) async-start(bf16[8,192,768]{2,1,0:T(8,128)(2,1)} %bitcast.55), calls=%async_computation.1 | async-start | bytes 4718592 | tf_op jit(solution)/shard_map/all_to_all | solution.py:405
  30.3 63.3 %all-gather.5.cloned.1.call-start = ((), (), s32[]{:S(2)}) async-start(), calls=%async_computation.9 | async-start | bytes 1474560 | tf_op jit(solution)/shard_map/all_gather | solution.py:379
  32.4 40.6 %copy-start.31 = (f32[512]{0:T(512)}, f32[512]{0:T(512)S(1)}, u32[]{:S(2)}) copy-start(f32[512]{0:T(512)S(1)} %get-tuple-element.99) | copy-start | bytes 6148
  32.4 40.6 %copy-start.15 = (f32[256,32]{0,1:T(8,128)}, f32[256,32]{0,1:T(8,128)S(1)}, u32[]{:S(2)}) copy-start(f32[256,32]{0,1:T(8,128)S(1)} %fusion.29) | copy-start | bytes 98308
  67.5 5.5 copy-start.25
  67.5 29.2 %copy-start.22 = (f32[768]{0:T(1024)}, f32[768]{0:T(1024)S(1)}, u32[]{:S(2)}) copy-start(f32[768]{0:T(1024)S(1)} %get-tuple-element.90) | copy-start | bytes 9220
  93.6 3.6 copy-start.10
  96.1 1.1 copy-start.5
  96.7 3.5 copy-start.35
  100.2 1.5 copy-start.4
  101.7 59.3 %all-to-all-start = ((bf16[8,192,768]{2,1,0:T(8,128)(2,1)}), bf16[8,192,768]{2,1,0:T(8,128)(2,1)S(1)}, u32[]{:S(2)}, u32[]{:S(2)}) async-start(bf16[8,192,768]{2,1,0:T(8,128)(2,1)} %bitcast.56), calls=%async_computation | async-start | bytes 4718592 | tf_op jit(solution)/shard_map/all_to_all | solution.py:405
  160.9 1.4 copy-start
  209.4 4.8 copy-start.1
  209.4 4.8 copy-start.14
  209.4 59.3 %all-to-all-start.4 = ((bf16[8,192,768]{2,1,0:T(8,128)(2,1)}), bf16[8,192,768]{2,1,0:T(8,128)(2,1)}, u32[]{:S(2)}, u32[]{:S(2)}) async-start(bf16[8,192,768]{2,1,0:T(8,128)(2,1)} %bitcast.57), calls=%async_computation.4 | async-start | bytes 4718592 | tf_op jit(solution)/shard_map/all_to_all | solution.py:405
  214.1 189.5 %reduce-scatter.4.cloned.1.call-start = ((), (), s32[]{:S(2)}) async-start(), calls=%async_computation.10 | async-start | bytes 6144000 | tf_op jit(solution)/shard_map/reduce_scatter | solution.py:468
  215.3 58.2 %copy-start.8 = (bf16[512,768]{1,0:T(8,128)(2,1)S(1)}, bf16[512,768]{1,0:T(8,128)(2,1)}, u32[]{:S(2)}) copy-start(bf16[512,768]{1,0:T(8,128)(2,1)} %param.15) | copy-start | bytes 2359300
  215.3 58.2 %copy-start.19 = (f32[512]{0:T(512)S(1)}, f32[512]{0:T(512)}, u32[]{:S(2)}) copy-start(f32[512]{0:T(512)} %copy-done.18) | copy-start | bytes 6148
  215.3 58.2 %copy-start.23 = (f32[768]{0:T(1024)S(1)}, f32[768]{0:T(1024)}, u32[]{:S(2)}) copy-start(f32[768]{0:T(1024)} %copy-done.22) | copy-start | bytes 9220
  215.3 58.2 %copy-start.34 = (f32[512]{0:T(512)S(1)}, f32[512]{0:T(512)}, u32[]{:S(2)}) copy-start(f32[512]{0:T(512)} %get-tuple-element.100) | copy-start | bytes 6148
  215.3 58.2 %copy-start.36 = (f32[512]{0:T(512)S(1)}, f32[512]{0:T(512)}, u32[]{:S(2)}) copy-start(f32[512]{0:T(512)} %copy-done.35) | copy-start | bytes 6148
  268.8 4.8 copy-start.6
  273.5 1.1 copy-start.13
  273.6 1.1 copy-start.20
  274.7 1.3 copy-start.38
  301.4 1.4 copy-start.12
  301.4 1.6 copy-start.11
  303.5 4.0 copy-start.16
  307.4 3.9 copy-start.17
  307.4 3.9 copy-start.28
  307.5 3.9 copy-start.29
  318.6 116.6 %reduce-scatter.8.cloned.1.call-start = ((), (), s32[]{:S(2)}) async-start(), calls=%async_computation.13 | async-start | bytes 5898240 | tf_op jit(solution)/shard_map/reduce_scatter | solution.py:437
  339.1 155.8 %reduce-scatter.6.cloned.1.call-start = ((), (), s32[]{:S(2)}) async-start(), calls=%async_computation.12 | async-start | bytes 5898240 | tf_op jit(solution)/shard_map/reduce_scatter | solution.py:436
  339.7 4.6 copy-start.37
  339.7 4.6 copy-start.27
  339.8 4.6 copy-start.30
  339.8 4.6 copy-start.33
  339.8 59.2 %all-to-all-start.3 = ((bf16[8,192,768]{2,1,0:T(8,128)(2,1)}), bf16[8,192,768]{2,1,0:T(8,128)(2,1)}, u32[]{:S(2)}, u32[]{:S(2)}) async-start(bf16[8,192,768]{2,1,0:T(8,128)(2,1)} %bitcast.53), calls=%async_computation.3 | async-start | bytes 4718592 | tf_op jit(solution)/shard_map/all_to_all | solution.py:405
  344.3 212.9 %all-reduce.7.cloned.1.call-start = ((), (), s32[]{:S(2)}) async-start(), calls=%async_computation.11 | async-start | bytes 2457600 | tf_op jit(solution)/shard_map/psum | solution.py:469
  344.4 54.6 %copy-start.21 = (f32[512]{0:T(512)S(1)}, f32[512]{0:T(512)}, u32[]{:S(2)}) copy-start(f32[512]{0:T(512)} %copy-done.18) | copy-start | bytes 6148
  557.2 2.5 copy-start.2
  (2 other events, 1.5 us)
Sparse Core Ops, SparseCore 0:
  12.5 51.5 all-gather.2
  66.0 27.6 all-gather.4
  318.7 56.5 reduce-scatter.3
  378.1 56.9 reduce-scatter.7
  438.0 56.9 reduce-scatter.5
  497.2 59.9 all-reduce.6

commit v2 on v1

--- a/solution.py
+++ b/solution.py
@@ -207,134 +207,312 @@
     )(qkv, qkv, qkv, d_attn, lse, rev, key_mask)
 
 
+def remote(src, dst, send, recv, dp, expert):
+    return pltpu.make_async_remote_copy(
+        src_ref=src, dst_ref=dst, send_sem=send, recv_sem=recv,
+        device_id={"dp": dp, "expert": expert}, device_id_type=pl.DeviceIdType.MESH,
+    )
+
+
+def greet(dp, expert, group, across):
+    barrier = pltpu.get_barrier_semaphore()
+
+    def hello(dp_to, expert_to):
+        pl.semaphore_signal(
+            barrier, inc=1, device_id={"dp": dp_to, "expert": expert_to}, device_id_type=pl.DeviceIdType.MESH
+        )
+
+    def one(k, carry):
+        hello(dp, lax.rem(expert + k, group))
+        return carry
+
+    lax.fori_loop(1, group, one, 0)
+    for flip in across:
+        hello(flipped(dp, flip), expert)
+    pl.semaphore_wait(barrier, group - 1 + len(across))
+
+
+def flipped(dp, flip):
+    low = lax.rem(dp, 2)
+    high = dp - low
+    if flip & 1:
+        low = 1 - low
+    if flip & 2:
+        high = 2 - high
+    return high + low
+
+
 def expert_kernel(
-    own_ref, x_ref, g_ref, other_ref, win_ref, wout_ref, wr_ref,
-    made_ref, drow_ref, act_ref, dpre_ref, dmade_ref, sel_ref, made_acc, drow_acc,
+    xb_ref, sel_ref, other_ref, wr_ref, g_hbm, win_hbm, wout_hbm,
+    dnorm_ref, made_hbm, gin_hbm, gout_ref, router_ref,
+    xs, xr, gr, db, win, wout, act, dpre, drow_acc, stage,
+    s_diag, s_x, s_y, r1x, r1y, r2x, r2y,
+    x_send, x_recv, d_send, d_recv, r_send, r_recv, load_sem, made_sem, out_sem,
+    *, group, chunks, step,
 ):
-    ff = win_ref.shape[1]
-    step = 1024
-    experts = wr_ref.shape[1] // 2
-    x = x_ref[...]
-    g = g_ref[...]
-    rows = x.shape[0]
-    logits = mm(x, wr_ref[...])
-    ids = lax.broadcasted_iota(jnp.int32, logits.shape, 1)
-    own = own_ref[0]
-    other = other_ref[...]
-    hit_own = ids == own
-    hit_other = ids == other
-    diff = jnp.sum(jnp.where(hit_other, logits, 0.0) - jnp.where(hit_own, logits, 0.0), axis=1, keepdims=True)
-    pair_own = 1.0 / (1.0 + jnp.exp(diff))
-    pair_other = 1.0 / (1.0 + jnp.exp(-diff))
-    g_wide = g.astype(f32)
-    d_made = (pair_own * g_wide).astype(bf16)
-    dmade_ref[...] = d_made
-
-    def body(i, carry):
-        cols = pl.ds(pl.multiple_of(i * step, step), step)
-        u = mm(x, win_ref[:, cols])
-        da = mm(d_made, wout_ref[:, cols])
-        u2 = u * u
-        h = 0.5 + 0.5 * jnp.tanh(u * (gelu_c + (gelu_c * gelu_k) * u2))
-        act = (u * h).astype(bf16)
-        slope = h + u * (2.0 * gelu_c + (6.0 * gelu_c * gelu_k) * u2) * (h - h * h)
-        dpre = (da * slope).astype(bf16)
-        act_ref[:, cols] = act
-        dpre_ref[:, cols] = dpre
-        m = mm(act, wout_ref[:, cols], 1, 1)
-        d = mm(dpre, win_ref[:, cols], 1, 1)
-
-        @pl.when(i == 0)
+    dp = lax.axis_index("dp")
+    me = lax.axis_index("expert")
+    width = xb_ref.shape[1]
+    ff = win.shape[1]
+    made_acc = dnorm_ref
+    cap = xs.shape[1]
+    cs = cap // chunks
+    rows = group * cs
+
+    loads = [
+        pltpu.make_async_copy(g_hbm, gr, load_sem.at[0]),
+        pltpu.make_async_copy(win_hbm, win, load_sem.at[1]),
+        pltpu.make_async_copy(wout_hbm, wout, load_sem.at[2]),
+    ]
+    for load in loads:
+        load.start()
+
+    def part(c):
+        return pl.ds(pl.multiple_of(c * cs, cs), cs)
+
+    def x_copy(c, k):
+        to = lax.rem(me + k, group)
+        return remote(xs.at[to, part(c)], xr.at[me, part(c)], x_send.at[c, k], x_recv.at[c, k], dp, to)
+
+    def d_copy(c, k):
+        to = lax.rem(me + k, group)
+        return remote(xs.at[to, part(c)], db.at[me, part(c)], d_send.at[c, k], d_recv.at[c, k], dp, to)
+
+    def over_peers(f):
+        def one(k, carry):
+            f(k)
+            return carry
+
+        lax.fori_loop(1, group, one, 0)
+
+    def made_copy(c, k):
+        src = s_x.at[pl.ds(pl.multiple_of(k * cs, cs), cs)]
+        return pltpu.make_async_copy(src, made_hbm.at[k, part(c)], made_sem.at[k])
+
+    def over_all(f):
+        def one(k, carry):
+            f(k)
+            return carry
+
+        lax.fori_loop(0, group, one, 0)
+
+    def pick(c, carry):
+        chosen = sel_ref[:, part(c), :].reshape(rows, sel_ref.shape[2])
+        xs[:, part(c), :] = mm(chosen, xb_ref[...]).astype(bf16).reshape(group, cs, width)
+
+        @pl.when(c == 0)
         def _():
-            made_acc[...] = m
-            drow_acc[...] = d
-
-        @pl.when(i > 0)
+            greet(dp, me, group, (1, 2))
+
+        over_peers(lambda k: x_copy(c, k).start())
+        xr[me, part(c), :] = xs[me, part(c), :]
+        return carry
+
+    lax.fori_loop(0, chunks, pick, 0)
+    for load in loads:
+        load.wait()
+    router_ref[...] = jnp.zeros_like(router_ref)
+
+    def work(c, carry):
+        over_peers(lambda k: x_copy(c, k).wait())
+        x = xr[:, part(c), :].reshape(rows, width)
+        g_wide = gr[:, part(c), :].reshape(rows, width).astype(f32)
+        logits = mm(x, wr_ref[...])
+        ids = lax.broadcasted_iota(jnp.int32, logits.shape, 1)
+        hit_own = ids == me
+        hit_other = ids == other_ref[:, part(c), :].reshape(rows, 1)
+        diff = jnp.sum(
+            jnp.where(hit_other, logits, 0.0) - jnp.where(hit_own, logits, 0.0), axis=1, keepdims=True
+        )
+        pair_own = 1.0 / (1.0 + jnp.exp(diff))
+        pair_other = 1.0 / (1.0 + jnp.exp(-diff))
+        d_made = (pair_own * g_wide).astype(bf16)
+
+        def body(i, inner):
+            cols = pl.ds(pl.multiple_of(i * step, step), step)
+            u = mm(x, win[:, cols])
+            da = mm(d_made, wout[:, cols])
+            u2 = u * u
+            h = 0.5 + 0.5 * jnp.tanh(u * (gelu_c + (gelu_c * gelu_k) * u2))
+            a = (u * h).astype(bf16)
+            slope = h + u * (2.0 * gelu_c + (6.0 * gelu_c * gelu_k) * u2) * (h - h * h)
+            d = (da * slope).astype(bf16)
+            act[:, part(c), cols] = a.reshape(group, cs, step)
+            dpre[:, part(c), cols] = d.reshape(group, cs, step)
+            m_part = mm(a, wout[:, cols], 1, 1)
+            d_part = mm(d, win[:, cols], 1, 1)
+
+            @pl.when(i == 0)
+            def _():
+                made_acc[...] = m_part
+                drow_acc[...] = d_part
+
+            @pl.when(i > 0)
+            def _():
+                made_acc[...] += m_part
+                drow_acc[...] += d_part
+
+            return inner
+
+        lax.fori_loop(0, ff // step, body, 0)
+        made = made_acc[...].astype(bf16).astype(f32)
+        d_gate = jnp.sum(g_wide * made, axis=1, keepdims=True)
+        push = pair_own * pair_other * d_gate
+        full = jnp.where(hit_own, push, 0.0) - jnp.where(hit_other, push, 0.0)
+        coarse = full.astype(bf16)
+        fine = full - coarse.astype(f32)
+        lanes = wr_ref.shape[1]
+        spread = (coarse.astype(f32) + pltpu.roll(fine, lanes // 2, 1)).astype(bf16)
+        router_ref[...] += mm(x, spread, 0, 0)
+        d_row = (drow_acc[...] + mm(coarse, wr_ref[...], 1, 1)).astype(bf16)
+        xs[:, part(c), :] = d_row.reshape(group, cs, width)
+        over_peers(lambda k: d_copy(c, k).start())
+        db[me, part(c), :] = xs[me, part(c), :]
+
+        @pl.when(c > 0)
         def _():
-            made_acc[...] += m
-            drow_acc[...] += d
-
+            over_all(lambda k: made_copy(c - 1, k).wait())
+
+        s_x[0:rows, :] = (pair_own * made).astype(bf16)
+        over_all(lambda k: made_copy(c, k).start())
+        gr[:, part(c), :] = d_made.reshape(group, cs, width)
         return carry
 
-    lax.fori_loop(0, ff // step, body, 0)
-    made = made_acc[...].astype(bf16).astype(f32)
-    made_ref[...] = (pair_own * made).astype(bf16)
-    d_gate = jnp.sum(g_wide * made, axis=1, keepdims=True)
-    push = pair_own * pair_other * d_gate
-    full = jnp.where(hit_own, push, 0.0) - jnp.where(hit_other, push, 0.0)
-    coarse = full.astype(bf16)
-    fine = (full - coarse.astype(f32)).astype(bf16)
-    lanes = wr_ref.shape[1]
-    fine_moved = pltpu.roll(fine.astype(f32), lanes // 2, 1)
-    sel = coarse.astype(f32) + fine_moved
-    sel = sel.astype(bf16)
-    sel_ref[...] = sel
-    back = mm(coarse, wr_ref[...], 1, 1)
-    drow_ref[...] = (drow_acc[...] + back).astype(bf16)
-
-
-def expert_pass(own, x_rows, g_rows, other, w_in, w_out, w_router):
-    rows, width = x_rows.shape
+    lax.fori_loop(0, chunks, work, 0)
+    over_all(lambda k: made_copy(chunks - 1, k).wait())
+
+    total_rows = group * cap
+    shard = ff // 4
+    half = width // 2
+    piece = shard // 2
+
+    def grad_cols(left, right, start):
+        a = left[...].reshape(total_rows, width)
+        b = right[:, :, pl.ds(start, piece)].reshape(total_rows, piece)
+        return mm(a, b, 0, 0)
+
+    def shard_into(dst, owner):
+        for p in range(2):
+            start = pl.multiple_of(owner * shard + p * piece, piece)
+            dst[:, p * piece : (p + 1) * piece] = grad_cols(gr, act, start).astype(dst.dtype)
+
+    px, py, pd = flipped(dp, 1), flipped(dp, 2), flipped(dp, 3)
+    upper, lower = slice(0, half), slice(half, width)
+    to_x1 = remote(s_diag.at[upper], r1x, r_send.at[0], r_recv.at[0], px, me)
+    to_y1 = remote(s_diag.at[lower], r1y, r_send.at[1], r_recv.at[1], py, me)
+    to_xa = remote(s_x.at[upper], r2x.at[upper], r_send.at[2], r_recv.at[2], px, me)
+    to_xb = remote(s_x.at[lower], r2x.at[lower], r_send.at[3], r_recv.at[3], px, me)
+    to_ya = remote(s_y.at[upper], r2y.at[upper], r_send.at[4], r_recv.at[4], py, me)
+    to_yb = remote(s_y.at[lower], r2y.at[lower], r_send.at[5], r_recv.at[5], py, me)
+    shard_into(s_diag, pd)
+    to_x1.start()
+    to_y1.start()
+    shard_into(s_x, px)
+    to_xa.start()
+    shard_into(s_y, py)
+    to_yb.start()
+
+    def out_copy(i):
+        slot = lax.rem(i, 2)
+        cols = pl.ds(pl.multiple_of(i * piece, piece), piece)
+        return pltpu.make_async_copy(stage.at[slot], gin_hbm.at[:, cols], out_sem.at[slot])
+
+    def in_grad(i, carry):
+        @pl.when(i >= 2)
+        def _():
+            out_copy(i - 2).wait()
+
+        x_all = xr[...].reshape(total_rows, width)
+        cols = pl.ds(pl.multiple_of(i * piece, piece), piece)
+        stage[lax.rem(i, 2)] = mm(x_all, dpre[:, :, cols].reshape(total_rows, piece), 0, 0).astype(bf16)
+        out_copy(i).start()
+        return carry
+
+    lax.fori_loop(0, 4, in_grad, 0)
+    to_y1.wait()
+    s_x[lower, :] = (s_x[lower, :].astype(f32) + r1y[...].astype(f32)).astype(bf16)
+    to_xb.start()
+    to_x1.wait()
+    s_y[upper, :] = (s_y[upper, :].astype(f32) + r1x[...].astype(f32)).astype(bf16)
+    to_ya.start()
+    lax.fori_loop(4, 8, in_grad, 0)
+    shard_into(gout_ref, dp)
+
+    def all_back(c, carry):
+        over_peers(lambda k: d_copy(c, k).wait())
+        return carry
+
+    lax.fori_loop(0, chunks, all_back, 0)
+    dnorm_ref[...] = mm(
+        sel_ref[...].reshape(total_rows, sel_ref.shape[2]), db[...].reshape(total_rows, width), 0, 0
+    )
+    for copy in (to_xa, to_xb, to_ya, to_yb):
+        copy.wait()
+    gout_ref[...] += r2x[...].astype(f32) + r2y[...].astype(f32)
+    out_copy(6).wait()
+    out_copy(7).wait()
+
+
+def expert_pass(xb, select, other, w_router, g_rows, w_in, w_out, chunks):
+    group, cap, tok_count = select.shape
+    width = xb.shape[1]
     ff = w_in.shape[1]
-    rt = 256
+    cs = cap // chunks
+    rows = group * cs
     lanes = w_router.shape[1]
-    row_block = pl.BlockSpec((rt, width), lambda r: (r, 0))
-    ff_block = pl.BlockSpec((rt, ff), lambda r: (r, 0))
-    once = dict(pipeline_mode=pl.Buffered(1))
+    shard = ff // 4
+    assert rows == tok_count and rows <= width
+    vmem = pl.BlockSpec(memory_space=pltpu.VMEM)
+    hbm = pl.BlockSpec(memory_space=pl.ANY)
+    block = (group, cap, width)
+    dma = pltpu.SemaphoreType.DMA
     return pl.pallas_call(
-        expert_kernel,
-        grid=(rows // rt,),
-        in_specs=[
-            pl.BlockSpec(memory_space=pltpu.SMEM),
-            row_block,
-            row_block,
-            pl.BlockSpec((rt, 1), lambda r: (r, 0)),
-            pl.BlockSpec((width, ff), lambda r: (0, 0), **once),
-            pl.BlockSpec((width, ff), lambda r: (0, 0), **once),
-            pl.BlockSpec((width, lanes), lambda r: (0, 0), **once),
+        functools.partial(expert_kernel, group=group, chunks=chunks, step=512),
+        in_specs=[vmem, vmem, vmem, vmem, hbm, hbm, hbm],
+        out_specs=[vmem, hbm, hbm, vmem, vmem],
+        out_shape=[
+            jax.ShapeDtypeStruct((tok_count, width), f32),
+            jax.ShapeDtypeStruct(block, bf16),
+            jax.ShapeDtypeStruct((width, ff), bf16),
+            jax.ShapeDtypeStruct((width, shard), f32),
+            jax.ShapeDtypeStruct((width, lanes), f32),
         ],
-        out_specs=[row_block, row_block, ff_block, ff_block, row_block, pl.BlockSpec((rt, lanes), lambda r: (r, 0))],
-        out_shape=[
-            jax.ShapeDtypeStruct((rows, width), bf16),
-            jax.ShapeDtypeStruct((rows, width), bf16),
-            jax.ShapeDtypeStruct((rows, ff), bf16),
-            jax.ShapeDtypeStruct((rows, ff), bf16),
-            jax.ShapeDtypeStruct((rows, width), bf16),
-            jax.ShapeDtypeStruct((rows, lanes), bf16),
+        scratch_shapes=[
+            pltpu.VMEM(block, bf16),
+            pltpu.VMEM(block, bf16),
+            pltpu.VMEM(block, bf16),
+            pltpu.VMEM(block, bf16),
+            pltpu.VMEM((width, ff), bf16),
+            pltpu.VMEM((width, ff), bf16),
+            pltpu.VMEM((group, cap, ff), bf16),
+            pltpu.VMEM((group, cap, ff), bf16),
+            pltpu.VMEM((rows, width), f32),
+            pltpu.VMEM((2, width, shard // 2), bf16),
+            pltpu.VMEM((width, shard), bf16),
+            pltpu.VMEM((width, shard), bf16),
+            pltpu.VMEM((width, shard), bf16),
+            pltpu.VMEM((width // 2, shard), bf16),
+            pltpu.VMEM((width // 2, shard), bf16),
+            pltpu.VMEM((width, shard), bf16),
+            pltpu.VMEM((width, shard), bf16),
+            dma((chunks, group)),
+            dma((chunks, group)),
+            dma((chunks, group)),
+            dma((chunks, group)),
+            dma((6,)),
+            dma((6,)),
+            dma((3,)),
+            dma((group,)),
+            dma((2,)),
         ],
-        scratch_shapes=[pltpu.VMEM((rt, width), f32), pltpu.VMEM((rt, width), f32)],
-        compiler_params=pltpu.CompilerParams(vmem_limit_bytes=56 << 20),
+        compiler_params=pltpu.CompilerParams(
+            collective_id=1, has_side_effects=True, vmem_limit_bytes=67_000_000
+        ),
         cost_estimate=pl.CostEstimate(
-            flops=8 * rows * width * ff, bytes_accessed=4 * rows * ff + 4 * width * ff, transcendentals=0
+            flops=12 * group * cap * width * ff, bytes_accessed=8 * width * ff, transcendentals=0
         ),
         name="expert_pass",
-    )(own, x_rows, g_rows, other, w_in, w_out, w_router)
-
-
-def weight_grad_kernel(x_ref, dm_ref, act_ref, dpre_ref, gin_ref, gout_ref):
-    gout_ref[...] = mm(dm_ref[...], act_ref[...], 0, 0).astype(bf16)
-    gin_ref[...] = mm(x_ref[...], dpre_ref[...], 0, 0).astype(bf16)
-
-
-def weight_grads(x_rows, d_made, act, d_pre):
-    rows, width = x_rows.shape
-    ff = act.shape[1]
-    ft = 512
-    full = pl.BlockSpec((rows, width), lambda f: (0, 0), pipeline_mode=pl.Buffered(1))
-    cols = pl.BlockSpec((rows, ft), lambda f: (0, f))
-    outs = pl.BlockSpec((width, ft), lambda f: (0, f))
-    return pl.pallas_call(
-        weight_grad_kernel,
-        grid=(ff // ft,),
-        in_specs=[full, full, cols, cols],
-        out_specs=[outs, outs],
-        out_shape=[jax.ShapeDtypeStruct((width, ff), bf16)] * 2,
-        compiler_params=pltpu.CompilerParams(vmem_limit_bytes=56 << 20),
-        cost_estimate=pl.CostEstimate(
-            flops=4 * rows * width * ff, bytes_accessed=4 * rows * ff + 4 * width * ff, transcendentals=0
-        ),
-        name="weight_grads",
-    )(x_rows, d_made, act, d_pre)
+    )(xb, select, other, w_router, g_rows, w_in, w_out)
 
 
 def rms_scale(vector):
@@ -361,7 +539,7 @@
     bucket_count = rel_bias.shape[1]
     expert_count = w_router.shape[1]
     assert w_in.shape[0] == 1 and expert_count == group and routes.shape[1] == 2
-    capacity = round_up(3 * tok_count * 2 // (2 * expert_count), 32)
+    capacity = 3 * tok_count * 2 // (2 * expert_count)
     rows = expert_count * capacity
 
     bias_cells = rel_bias.size
@@ -397,17 +575,15 @@
     slots = jnp.arange(capacity, dtype=jnp.int32)
     select = (rank.T[:, None, :] == slots[None, :, None]).astype(bf16).reshape(rows, tok_count)
     both = jnp.sum(routes, axis=1)
-    other_tok = (both[:, None] - expert_ids[None, :]) * hot.astype(jnp.int32) - (1 - hot.astype(jnp.int32))
     chosen = rank.T[:, None, :] == slots[None, :, None]
     other_slot = jnp.sum(jnp.where(chosen, both[None, None, :], 0), axis=2) - expert_ids[:, None]
 
     def to_experts(block):
-        return lax.all_to_all(
-            block.reshape((group, capacity) + block.shape[1:]), "expert", split_axis=0, concat_axis=0, tiled=True
-        ).reshape(block.shape)
-
-    g_rows = to_experts(jnp.dot(select, cotangent, preferred_element_type=f32).astype(bf16))
-    other = to_experts(other_slot.reshape(rows, 1))
+        return lax.all_to_all(block, "expert", split_axis=0, concat_axis=0, tiled=True)
+
+    g_rows = jnp.dot(select, cotangent, preferred_element_type=f32).astype(bf16)
+    g_rows = to_experts(g_rows.reshape(group, capacity, model_width))
+    other = to_experts(other_slot.reshape(group, capacity, 1))
 
     distances = (2 * tile - jnp.arange(2 * tile, dtype=jnp.int32)) % (2 * tile)
     bucket_hot = (bucket_of(distances)[:, None] == jnp.arange(bucket_count)).astype(f32)
@@ -423,25 +599,21 @@
     scale_second = rms_scale(hidden)
     normed_moe = (hidden * scale_second * gain_second).astype(bf16)
 
-    x_rows = to_experts(jnp.dot(select, normed_moe, preferred_element_type=f32).astype(bf16))
     lanes = max(tile, 2 * expert_count)
     w_gate_wide = jnp.zeros((model_width, lanes), bf16).at[:, :expert_count].set(w_gate)
-    own = lax.axis_index("expert").astype(jnp.int32).reshape(1)
-    made, d_rows, act, d_pre, d_made, sel = expert_pass(
-        own, x_rows, g_rows, other, w_in[0], w_out[0], w_gate_wide
-    )
-    d_back = to_experts(d_rows)
-    made_back = to_experts(made)
-    full_in, full_out = weight_grads(x_rows, d_made, act, d_pre)
+    chunks = 3
+    d_normed, made, full_in, grad_w_out, router_wide = expert_pass(
+        normed_moe, select.reshape(expert_count, capacity, tok_count), other, w_gate_wide, g_rows,
+        w_in[0], w_out[0], chunks,
+    )
+    made_back = to_experts(made).reshape(rows, model_width)
     grad_w_in = lax.psum_scatter(full_in, "dp", scatter_dimension=1, tiled=True).astype(f32)[None]
-    grad_w_out = lax.psum_scatter(full_out, "dp", scatter_dimension=1, tiled=True).astype(f32)[None]
-    router_wide = jnp.dot(x_rows.T, sel, preferred_element_type=f32)
+    grad_w_out = grad_w_out[None]
     grad_router = router_wide[:, :expert_count] + router_wide[:, lanes // 2 : lanes // 2 + expert_count]
 
     moe_out = jnp.dot(select.T, made_back, preferred_element_type=f32)
     outputs = (valid_mask * (hidden + moe_out)).astype(bf16)
 
-    d_normed = jnp.dot(select.T, d_back, preferred_element_type=f32)
     d_hidden_norm, grad_gain_moe = rms_back(hidden, scale_second, gain_second, d_normed)
     d_hidden = cotangent.astype(f32) * valid_mask + d_hidden_norm
     d_proj = (d_hidden * valid_mask).astype(bf16)

time: 572 us -> 484 us (0.85)
  waiting for transfers between devices: 339 us -> 195 us
  Pallas kernels: 103 us -> 158 us
  matrix products: 33.6 us -> 25.9 us
    all_to_all x5 -> x3, waiting for transfers between devices: 157 us -> 3.42 us  [to_experts(): lax.all_to_all(block, 'expert', split_axis=0, concat_axis=0, tiled=True)]
    pallas_call x2 -> x1, Pallas kernels: 67.4 us -> 123 us  [expert_pass(): pl.pallas_call(functools.partial(expert_kernel, group=group, chunks=chunk...]
    reduce_scatter x1, waiting for transfers between devices: 0.01 us -> 49.7 us  [on_device(): part = lax.psum_scatter(packed, 'dp', scatter_dimension=0, tiled=True)]
    reduce_scatter x1 -> x0, waiting for transfers between devices: 31.5 us -> none  [on_device(): lax.psum_scatter(full_out, 'dp', scatter_dimension=1, tiled=True)]
    dot_general x4 -> x1, matrix products: 10.4 us -> 2.8 us  [on_device(): g_rows = jnp.dot(select, cotangent, preferred_element_type=f32).astype(bf16)]
    all_to_all x5 -> x3, starting transfers between devices: 24 us -> 26.7 us  [to_experts(): lax.all_to_all(block, 'expert', split_axis=0, concat_axis=0, tiled=True)]
  transfers between devices with their start and end apart: 11 -> 8, of which waited for: 9 -> 6; matrix products, arithmetic and copies ran while one was open for 7% -> 7% of each run, Pallas kernels for 7% -> 4%
where the time goes in v2:
time: 484 us; the launch traced here: 480 us
  waiting for transfers between devices  195 us (40%)
  Pallas kernels  158 us (33%)
  other arithmetic  30.9 us (6%)
  starting transfers between devices  27.7 us (6%)
  local copies, waits for them, and re-layouts  26.7 us (6%)
  matrix products  25.9 us (5%)
  between operations  15 us (3%)
    pallas_call x1, Pallas kernels, expert_pass(): pl.pallas_call(functools.partial(expert_kernel, group=group, chunks=chunk...  123 us
    psum x1, waiting for transfers between devices, on_device(): whole = lax.psum(part, 'expert').astype(f32)  59.3 us
    reduce_scatter x1, waiting for transfers between devices, on_device(): lax.psum_scatter(full_in, 'dp', scatter_dimension=1, tiled=True).astype(f32)  54.5 us
    reduce_scatter x1, waiting for transfers between devices, on_device(): part = lax.psum_scatter(packed, 'dp', scatter_dimension=0, tiled=True)  49.7 us
    all_gather x1, waiting for transfers between devices, on_device(): lax.all_gather(jnp.concatenate([w_qkv, small], axis=1), 'dp', axis=0, til...  26.8 us
    all_to_all x3, starting transfers between devices, to_experts(): lax.all_to_all(block, 'expert', split_axis=0, concat_axis=0, tiled=True)  26.7 us
    pallas_call x1, Pallas kernels, attention_forward(): pl.pallas_call(attn_fwd_kernel, grid=(pairs,), in_specs=[pl.BlockSpec((co...  18.8 us
    pallas_call x1, Pallas kernels, attention_backward(): pl.pallas_call(attn_bwd_kernel, grid=(pairs,), in_specs=[block, pl.BlockS...  17 us
  transfers between devices with their start and end apart: 8, of which 6 were waited for; matrix products, arithmetic and copies ran while one was open for 7% of the time, Pallas kernels for 4%

profile of v2, /device:TPU:0, one launch (start us, length us, event | category | flops | bytes accessed | tf_op | source)
XLA Modules:
  0.0 479.6 jit_solution(16226358996755754264)
XLA Ops:
  10.2 2.2 fusion.22
  14.4 6.4 %all-to-all-start = ((s32[8,192,1]{1,2,0:T(1,128)}), s32[8,192,1]{1,2,0:T(1,128)S(1)}, u32[]{:S(2)}, u32[]{:S(2)}) async-start(s32[8,192,1]{1,2,0:T(1,128)} %copy.47), calls=%async_computation | async-start | bytes 16384 | tf_op jit(solution)/shard_map/all_to_all | solution.py:582
  21.4 2.8 convolution_convert_fusion.2
  24.2 2.2 all-to-all-done
  26.4 4.5 all-to-all-start.1
  34.4 1.7 fusion.3.sel_ref
  36.1 1.2 copy.48.other_ref
  37.3 26.8 %all-gather.3.cloned.1.call-done = bf16[768,2432]{1,0:T(8,128)(2,1)} async-done(((bf16[192,2432]{1,0:T(8,128)(2,1)}), bf16[768,2432]{1,0:T(8,128)(2,1)}) %all-gather.3.cloned.1.call-update) | async-done | bytes 3735568 | tf_op jit(solution)/shard_map/all_gather | solution.py:556
  64.1 1.1 slice_reduce_fusion
  66.2 1.6 slice_select_fusion
  68.5 1.3 convert_reduce_fusion
  69.9 5.5 %convolution_convert_fusion.1.q_ref.k_ref.v_ref = bf16[512,2304]{1,0:T(8,128)(2,1)} fusion(bf16[768,2432]{1,0:T(8,128)(2,1)} %all-gather.3.cloned.1.call-done, bf16[512,768]{1,0:T(8,128)(2,1)S(1)} %copy-done.4, f32[768]{0:T(1024)S(1)} %get-tuple-element.85, f32[512]{0:T(512)S(1)} %get-tuple-element.95), kind=kOutput, calls=%fused_computation.4 | convolution fusion | flops 1814691840 | bytes 6689792 | tf_op jit(solution)/shard_map/dot_general | solution.py:596
  75.4 18.8 %attn_fwd.1 = (bf16[512,768]{1,0:T(8,128)(2,1)}, f32[6,512,128]{2,1,0:T(8,128)}) custom-call(bf16[512,2304]{1,0:T(8,128)(2,1)} %convolution_convert_fusion.1.q_ref.k_ref.v_ref, bf16[512,2304]{1,0:T(8,128)(2,1)} %convolution_convert_fusion.1.q_ref.k_ref.v_ref, bf16[512,2304]{1,0:T(8,128)(2,1)} %convolution_convert_fusion.1.q_ref.k_ref.v_ref, ...), custom_call_target="tpu_custom_call" | custom-call | flops 805306368 | bytes 6291456 | tf_op jit(solution)/shard_map/attn_fwd/pallas_call | solution.py:88
  94.2 2.4 multiply_reduce_fusion.2
  96.6 1.2 copy-done
  97.8 1.1 multiply_convert_fusion.1.xb_ref
  98.8 122.6 %expert_pass.1 = (f32[512,768]{1,0:T(8,128)}, bf16[8,192,768]{2,1,0:T(8,128)(2,1)}, bf16[768,3072]{1,0:T(8,128)(2,1)}, f32[768,768]{1,0:T(8,128)}, f32[768,128]{1,0:T(8,128)}) custom-call(bf16[512,768]{1,0:T(8,128)(2,1)} %multiply_convert_fusion.1.xb_ref, bf16[8,192,512]{2,1,0:T(8,128)(2,1)} %fusion.3.sel_ref, s32[8,192,1]{2,1,0:T(8,128)} %copy.48.other_ref, ...), custom_call_target="tpu_custom_call" | custom-call | flops 43486543872 | bytes 18874368 | tf_op jit(solution)/shard_map/expert_pass/pallas_call | solution.py:469
  221.4 2.5 multiply_reduce_fusion
  224.5 1.7 subtract_add_fusion
  226.2 1.9 convolution_convert_fusion.3
  228.1 1.7 convolution_convert_fusion.4.do_ref
  229.9 17.0 %attn_bwd.1 = (bf16[512,768]{1,0:T(8,128)(2,1)}, bf16[512,768]{1,0:T(8,128)(2,1)}, bf16[512,768]{1,0:T(8,128)(2,1)}, f32[6,2,256]{2,1,0:T(2,128)}) custom-call(bf16[512,2304]{1,0:T(8,128)(2,1)} %convolution_convert_fusion.1.q_ref.k_ref.v_ref, bf16[512,2304]{1,0:T(8,128)(2,1)} %convolution_convert_fusion.1.q_ref.k_ref.v_ref, ...), custom_call_target="tpu_custom_call" | custom-call | flops 2013265920 | bytes 7864320 | tf_op jit(solution)/shard_map/attn_bwd/pallas_call | solution.py:187
  246.8 1.3 mul.238
  248.1 1.5 multiply_reduce_fusion.3
  249.6 1.3 reshape.247
  251.0 1.3 pad.23
  252.2 1.3 reshape.248
  253.6 1.0 fusion.46
  254.6 1.1 copy.51
  255.7 1.1 copy.50
  256.8 1.3 constant_dynamic-update-slice_fusion.2
  258.5 0.9 copy-done.5
  259.4 3.9 convolution_convert_fusion
  263.3 3.3 fusion.11
  266.9 5.5 %fusion.1 = bf16[768,3200]{1,0:T(8,128)(2,1)} fusion(bf16[768,11]{1,0:T(8,128)(2,1)S(1)} %copy.52, bf16[768,768]{1,0:T(8,128)(2,1)} %convolution_convert_fusion.3, bf16[768,2304]{1,0:T(8,128)(2,1)} %convolution_convert_fusion), kind=kLoop, calls=%fused_computation.3 | loop fusion | flops 19660800 | bytes 9650688 | tf_op jit(solution)/shard_map/concatenate | solution.py:639
  272.9 15.9 %all-to-all-start.2 = ((bf16[8,192,768]{2,1,0:T(8,128)(2,1)}), bf16[8,192,768]{2,1,0:T(8,128)(2,1)}, u32[]{:S(2)}, u32[]{:S(2)}) async-start(bf16[8,192,768]{2,1,0:T(8,128)(2,1)} %get-tuple-element.34), calls=%async_computation.2 | async-start | bytes 4718592 | tf_op jit(solution)/shard_map/all_to_all | solution.py:582
  289.1 3.5 fusion.16
  292.7 49.7 %reduce-scatter.3.cloned.1.call-done = bf16[192,3200]{1,0:T(8,128)(2,1)} async-done(((bf16[768,3200]{1,0:T(8,128)(2,1)}), bf16[192,3200]{1,0:T(8,128)(2,1)}) %reduce-scatter.3.cloned.1.call-update) | async-done | bytes 1228816 | tf_op jit(solution)/shard_map/reduce_scatter | solution.py:640
  342.3 1.2 all-to-all-done.2
  343.6 4.2 fusion.19
  347.7 54.5 %reduce-scatter.5.cloned.1.call-done = bf16[768,768]{1,0:T(8,128)(2,1)} async-done(((bf16[768,3072]{1,0:T(8,128)(2,1)}), bf16[768,768]{1,0:T(8,128)(2,1)}) %reduce-scatter.5.cloned.1.call-update) | async-done | bytes 1179664 | tf_op jit(solution)/shard_map/reduce_scatter | solution.py:610
  402.2 2.8 bitcast_convert_fusion
  405.0 59.3 %all-reduce.7.cloned.1.call-done = bf16[192,3200]{1,0:T(8,128)(2,1)} async-done(((bf16[192,3200]{1,0:T(8,128)(2,1)}), bf16[192,3200]{1,0:T(8,128)(2,1)}) %all-reduce.7.cloned.1.call-update) | async-done | bytes 1228816 | tf_op jit(solution)/shard_map/psum | solution.py:641
  464.4 1.5 convert_element_type.284
  468.2 0.9 slice.89
  469.1 1.3 slice.88
  470.4 1.0 copy-done.6
  471.4 1.4 copy.62
  (104 shorter events, 14.4 us)
Async XLA Ops:
  7.2 5.9 %copy-start.16 = (s32[512,2]{0,1:T(2,128)S(1)}, s32[512,2]{0,1:T(2,128)}, u32[]{:S(2)}) copy-start(s32[512,2]{0,1:T(2,128)} %param.17) | copy-start | bytes 12292
  7.2 56.9 %all-gather.3.cloned.1.call-start = ((), (), s32[]{:S(2)}) async-start(), calls=%async_computation.5 | async-start | bytes 4669440 | tf_op jit(solution)/shard_map/all_gather | solution.py:556
  10.2 11.2 %copy-start.8 = (bf16[512,768]{1,0:T(8,128)(2,1)S(1)}, bf16[512,768]{1,0:T(8,128)(2,1)}, u32[]{:S(2)}) copy-start(bf16[512,768]{1,0:T(8,128)(2,1)} %param.15) | copy-start | bytes 2359300
  14.4 12.0 %all-to-all-start = ((s32[8,192,1]{1,2,0:T(1,128)}), s32[8,192,1]{1,2,0:T(1,128)S(1)}, u32[]{:S(2)}, u32[]{:S(2)}) async-start(s32[8,192,1]{1,2,0:T(1,128)} %copy.47), calls=%async_computation | async-start | bytes 16384 | tf_op jit(solution)/shard_map/all_to_all | solution.py:582
  26.4 6.5 %copy-start.4 = (bf16[512,768]{1,0:T(8,128)(2,1)S(1)}, bf16[512,768]{1,0:T(8,128)(2,1)}, u32[]{:S(2)}) copy-start(bf16[512,768]{1,0:T(8,128)(2,1)} %param.14) | copy-start | bytes 2359300
  26.4 72.5 %all-to-all-start.1 = ((bf16[8,192,768]{2,1,0:T(8,128)(2,1)}), bf16[8,192,768]{2,1,0:T(8,128)(2,1)}, u32[]{:S(2)}, u32[]{:S(2)}) async-start(bf16[8,192,768]{2,1,0:T(8,128)(2,1)} %bitcast.4), calls=%async_computation.1 | async-start | bytes 4718592 | tf_op jit(solution)/shard_map/all_to_all | solution.py:582
  30.9 63.3 %all-gather.5.cloned.1.call-start = ((), (), s32[]{:S(2)}) async-start(), calls=%async_computation.6 | async-start | bytes 1474560 | tf_op jit(solution)/shard_map/all_gather | solution.py:557
  31.6 310.7 %reduce-scatter.3.cloned.1.call-start = ((), (), s32[]{:S(2)}) async-start(), calls=%async_computation.7 | async-start | bytes 6144000 | tf_op jit(solution)/shard_map/reduce_scatter | solution.py:640
  32.9 195.2 %copy-start.14 = (f32[512]{0:T(512)}, f32[512]{0:T(512)S(1)}, u32[]{:S(2)}) copy-start(f32[512]{0:T(512)S(1)} %fusion.45) | copy-start | bytes 6148
  33.7 36.1 %copy-start.22 = (f32[512]{0:T(512)}, f32[512]{0:T(512)S(1)}, u32[]{:S(2)}) copy-start(f32[512]{0:T(512)S(1)} %get-tuple-element.95) | copy-start | bytes 6148
  33.7 34.8 %copy-start.12 = (f32[256,32]{0,1:T(8,128)}, f32[256,32]{0,1:T(8,128)S(1)}, u32[]{:S(2)}) copy-start(f32[256,32]{0,1:T(8,128)S(1)} %fusion.25) | copy-start | bytes 98308
  69.8 5.5 %copy-start.17 = (f32[768]{0:T(1024)}, f32[768]{0:T(1024)S(1)}, u32[]{:S(2)}) copy-start(f32[768]{0:T(1024)S(1)} %get-tuple-element.85) | copy-start | bytes 9220
  96.6 1.2 copy-start
  221.4 3.1 copy-start.1
  221.4 3.1 copy-start.3
  224.5 1.7 copy-start.11
  226.2 1.9 copy-start.24
  229.9 23.7 %copy-start.7 = (f32[768,128]{1,0:T(8,128)S(1)}, f32[768,128]{1,0:T(8,128)}, u32[]{:S(2)}) copy-start(f32[768,128]{1,0:T(8,128)} %get-tuple-element.40) | copy-start | bytes 1179652
  256.8 1.4 copy-start.10
  256.8 1.6 copy-start.9
  258.2 1.2 copy-start.5
  258.2 1.2 copy-start.18
  258.2 1.2 copy-start.23
  259.4 3.9 copy-start.13
  263.3 3.3 copy-start.19
  263.3 3.3 copy-start.20
  272.3 129.8 %reduce-scatter.5.cloned.1.call-start = ((), (), s32[]{:S(2)}) async-start(), calls=%async_computation.9 | async-start | bytes 5898240 | tf_op jit(solution)/shard_map/reduce_scatter | solution.py:610
  272.9 16.2 %copy-start.21 = (f32[512]{0:T(512)S(1)}, f32[512]{0:T(512)}, u32[]{:S(2)}) copy-start(f32[512]{0:T(512)} %get-tuple-element.94) | copy-start | bytes 6148
  272.9 70.6 %all-to-all-start.2 = ((bf16[8,192,768]{2,1,0:T(8,128)(2,1)}), bf16[8,192,768]{2,1,0:T(8,128)(2,1)}, u32[]{:S(2)}, u32[]{:S(2)}) async-start(bf16[8,192,768]{2,1,0:T(8,128)(2,1)} %get-tuple-element.34), calls=%async_computation.2 | async-start | bytes 4718592 | tf_op jit(solution)/shard_map/all_to_all | solution.py:582
  288.8 175.6 %all-reduce.7.cloned.1.call-start = ((), (), s32[]{:S(2)}) async-start(), calls=%async_computation.8 | async-start | bytes 2457600 | tf_op jit(solution)/shard_map/psum | solution.py:641
  289.1 54.4 %copy-start.15 = (f32[512]{0:T(512)S(1)}, f32[512]{0:T(512)}, u32[]{:S(2)}) copy-start(f32[512]{0:T(512)} %copy-done.14) | copy-start | bytes 6148
  464.4 2.5 copy-start.2
  469.1 2.3 copy-start.6
Sparse Core Ops, SparseCore 0:
  12.5 51.5 all-gather.2
  66.0 27.6 all-gather.4
  272.5 69.8 reduce-scatter.2
  345.2 56.9 reduce-scatter.4
  404.4 59.9 all-reduce.6
